TPU v7x, 16 devices: a whole 2x2x2 slice. The times are simulated.
16 devices in a mesh: dp: 4 (over z, y), cp: 4 (over x, core).
Axes of the slice: x: 2, y: 2, z: 2, core: 2. Of those that a mesh axis runs over, the one named last changes fastest.
Arguments:
- hidden: bfloat16 [128, 8, 1024], P('dp'), parts along dimension 0
- memory: bfloat16 [128, 1024, 1024], P('dp', 'cp'), parts along dimension 0
- ln_gain: bfloat16 [1024], replicated
- ln_bias: bfloat16 [1024], replicated
- w_q: bfloat16 [1024, 1024], replicated
- b_q: bfloat16 [1024], replicated
- w_k: bfloat16 [1024, 1024], replicated
- w_v: bfloat16 [1024, 1024], replicated
- b_v: bfloat16 [1024], replicated
- w_o: bfloat16 [1024, 1024], replicated
- b_o: bfloat16 [1024], replicated
- grad_y: bfloat16 [128, 8, 1024], P('dp'), parts along dimension 0
Outputs:
- output 1: bfloat16 [128, 8, 1024], P('dp'), parts along dimension 0
- output 2: bfloat16 [128, 8, 1024], P('dp'), parts along dimension 0
- output 3: bfloat16 [128, 1024, 1024], P('dp', 'cp'), parts along dimension 0
- output 4: float32 [4096], P('dp'), parts along dimension 0
- output 5: float32 [4096], P('dp'), parts along dimension 0
- output 6: float32 [4096, 1024], P('dp'), parts along dimension 0
- output 7: float32 [4096], P('dp'), parts along dimension 0
- output 8: float32 [4096, 1024], P('dp'), parts along dimension 0
- output 9: float32 [4096, 1024], P('dp'), parts along dimension 0
- output 10: float32 [4096], P('dp'), parts along dimension 0
- output 11: float32 [4096, 1024], P('dp'), parts along dimension 0
- output 12: float32 [4096], P('dp'), parts along dimension 0
There are 4 independent parts. A program takes and returns all parts, laid end to end along the dimension named above; an argument that names none is the same for every part.
All inputs are finite; a program needn't handle non-finite values.
Results may differ from a plain program's by a relative error of at most 0.00976275.
Values are sent between devices in bfloat16 or wider.
A program may use at most 1 GiB of HBM per device.

v0:
```python
import functools

import jax
import jax.numpy as jnp
from jax import lax
from jax.experimental import pallas as pl
from jax.experimental.pallas import tpu as pltpu
from jax.sharding import PartitionSpec as P


EPS = 1e-5
HEAD = 64
PAIR = 2 * HEAD
F32 = jnp.float32
BF16 = jnp.bfloat16
NT = (((1,), (1,)), ((), ()))
TN = (((0,), (0,)), ((), ()))
NN = (((1,), (0,)), ((), ()))
VMEM_LIMIT = 67043328


def dot(a, b, dims):
    return lax.dot_general(a, b, dims, preferred_element_type=F32)


def split_heads(x, n_seq):
    x = x.reshape(n_seq, x.shape[0] // n_seq, PAIR)
    low = lax.broadcasted_iota(jnp.int32, x.shape, 2) < HEAD
    zero = jnp.zeros_like(x)
    both = jnp.concatenate([jnp.where(low, x, zero), jnp.where(low, zero, x)], axis=1)
    return both.astype(BF16).reshape(-1, PAIR)


def join_heads(x, n_seq):
    n_tok = x.shape[0] // (2 * n_seq)
    x = x.reshape(n_seq, 2 * n_tok, PAIR)
    low = lax.broadcasted_iota(jnp.int32, (n_seq, n_tok, PAIR), 2) < HEAD
    return jnp.where(low, x[:, :n_tok], x[:, n_tok:]).reshape(n_seq * n_tok, PAIR)


def normalize(h_ref, vec_ref, x_scr):
    h = h_ref[...].astype(F32)
    c = h - jnp.mean(h, axis=-1, keepdims=True)
    inv = lax.rsqrt(jnp.mean(c * c, axis=-1, keepdims=True) + EPS)
    x_scr[...] = (c * inv * vec_ref[0:1, :] + vec_ref[1:2, :]).astype(BF16)


def pair_of(vec_ref, row, i):
    return vec_ref[row:row + 1, pl.ds(pl.multiple_of(i * PAIR, PAIR), PAIR)]


def place(out_ref, part, i, x, weight):
    step = 256
    for j in range(0, out_ref.shape[3], step):
        out_ref[part, i, :, j:j + step] = dot(x, weight(j, step), NT).astype(BF16)


def send(src, dst, sems, k, peer):
    return pltpu.make_async_remote_copy(
        src_ref=src, dst_ref=dst, send_sem=sems[0].at[k], recv_sem=sems[1].at[k],
        device_id={"cp": peer}, device_id_type=pl.DeviceIdType.MESH)


def fused_kernel(scale, n_cp, h_ref, gy_ref, wq_ref, wk_ref, wv_ref, wo_ref, m_ref, gain_ref, bias_ref, bq_ref, bv_ref,
                 pg_ref, chip0_ref, chip1_ref, chip2_ref, chip3_ref, oq_ref, q2_out, d2_out, small_ref,
                 x_scr, gy_scr, vec_scr, zg_scr, m_scr, e_scr, dp_scr, wk_scr, wv_scr, ps_scr, q2_scr, d2_scr, st_scr, other,
                 mine_oq, theirs_oq, got_oq, keep_x, give_x, got_x, full_oq, small_scr, got_dw,
                 in_sem, w_sem, m_sem, q_sem, chip_sem, out_sem, pg_sem, pg_scr,
                 st_s, st_r, rd_s, rd_r, rx_s, rx_r, ax_s, ax_r, ad_s, ad_r, dw_s, dw_r, sm_s, sm_r):
    _, n_pairs, n_rows, width = zg_scr.shape
    n_seq, n_fr, _ = m_scr.shape
    n_row = n_rows // n_seq
    rows = n_row * n_pairs
    n_blk = n_seq // n_pairs
    quarter = keep_x.shape[2]
    halves = [slice(0, n_pairs // 2), slice(n_pairs // 2, n_pairs)]
    me = lax.axis_index("cp")
    core = lax.rem(me, 2)
    chip = lax.div(me, 2)
    mate = me + 1 - 2 * core
    across = me + 2 - 4 * chip
    first = core == 0
    left = chip == 0
    peers = [lax.rem(me + d, n_cp) for d in range(1, n_cp)]
    wq_at, wo_at = n_seq - 2 * n_blk, n_seq - n_blk
    per_row = n_fr // PAIR

    def cols(k):
        return pl.ds(pl.multiple_of(k * PAIR, PAIR), PAIR)

    def seq_rows(b):
        return pl.ds(pl.multiple_of(b * n_row, n_row), n_row)

    def wo_rows(k):
        return lax.div(k, per_row), pl.ds(pl.multiple_of(lax.rem(k, per_row) * PAIR, PAIR), PAIR)

    def weight_copies(k):
        c = cols(k)
        block, r = wo_rows(k)
        return [pltpu.make_async_copy(wq_ref.at[:, :, c], m_scr.at[wq_at:wo_at, :, c], w_sem.at[0, k]),
                pltpu.make_async_copy(wo_ref.at[block, r, :], m_scr.at[wo_at + block, r, :], w_sem.at[1, k]),
                pltpu.make_async_copy(wk_ref.at[:, c], wk_scr.at[:, c], w_sem.at[2, k]),
                pltpu.make_async_copy(wv_ref.at[:, c], wv_scr.at[:, c], w_sem.at[3, k])]

    def mem_copy(g):
        at = pl.ds(g * n_blk, n_blk)
        return pltpu.make_async_copy(m_ref.at[at], m_scr.at[at], m_sem.at[g])

    def act_copies():
        return [pltpu.make_async_copy(h_ref, x_scr, in_sem.at[0]), pltpu.make_async_copy(gy_ref, gy_scr, in_sem.at[1])]

    def q_copies():
        return [pltpu.make_async_copy(q2_scr, q2_out, q_sem.at[0]), pltpu.make_async_copy(d2_scr, d2_out, q_sem.at[1])]

    def chip_copies(k):
        out, at = [], 0
        for n, ref in enumerate((chip0_ref, chip1_ref, chip2_ref, chip3_ref)):
            out.append(pltpu.make_async_copy(e_scr.at[k, at:at + ref.shape[0], :], ref.at[:, cols(k)], chip_sem.at[n, k]))
            at += ref.shape[0]
        return out

    def out_copies():
        return [pltpu.make_async_copy(full_oq.at[k, p], oq_ref.at[p, :, k * PAIR:(k + 1) * PAIR], out_sem.at[p, k])
                for k in range(n_pairs) for p in range(2)]

    def pg_copy(g):
        slot = lax.rem(g, 2)
        return pltpu.make_async_copy(pg_scr.at[slot], pg_ref.at[pl.ds(g * n_blk, n_blk)], pg_sem.at[slot])

    def stats_copy(k):
        return send(st_scr, other.at[k], (st_s, st_r), k, peers[k])

    def oq_mate(h):
        return send(theirs_oq.at[halves[h]], got_oq.at[halves[h]], (rd_s, rd_r), h, mate)

    def oq_across(h):
        return send(give_x.at[halves[h]], got_x.at[halves[h]], (rx_s, rx_r), h, across)

    def own_across(h):
        at = pl.ds(pl.multiple_of((2 * core + chip) * quarter, quarter), quarter)
        return send(full_oq.at[halves[h], :, at, :], full_oq.at[halves[h], :, at, :], (ax_s, ax_r), h, across)

    def half_mate(h):
        at = pl.ds(pl.multiple_of(core * 2 * quarter, quarter), 2 * quarter)
        return send(full_oq.at[halves[h], :, at, :], full_oq.at[halves[h], :, at, :], (ad_s, ad_r), h, mate)

    def dw_mate(k):
        return send(dp_scr.at[k], got_dw.at[k], (dw_s, dw_r), k, mate)

    def small_copy(k):
        return send(small_scr.at[me], small_scr.at[me], (sm_s, sm_r), k, peers[k])

    def add_mate(h):
        oq_mate(h).wait()
        t = mine_oq[halves[h]] + got_oq[halves[h]]
        top, bottom = t[:, :, :quarter], t[:, :, quarter:]
        keep_x[halves[h]] = jnp.where(left, top, bottom)
        give_x[halves[h]] = jnp.where(left, bottom, top)

    def finish(h):
        oq_across(h).wait()
        t = keep_x[halves[h]] + got_x[halves[h]]
        at = pl.ds(pl.multiple_of((2 * core + chip) * quarter, quarter), quarter)
        full_oq[halves[h], :, at, :] = t.astype(BF16)
        small_scr[me, 0, halves[h], :] = jnp.sum(t[:, 1], axis=1)

    for c in act_copies():
        c.start()

    @pl.loop(0, n_pairs)
    def _(k):
        for c in weight_copies(k):
            c.start()

    barrier = pltpu.get_barrier_semaphore()
    for peer in peers:
        pl.semaphore_signal(barrier, inc=1, device_id={"cp": peer}, device_id_type=pl.DeviceIdType.MESH)
    for k, ref in enumerate((gain_ref, bias_ref, bq_ref, bv_ref)):
        vec_scr[k:k + 1, :] = ref[...].astype(F32).reshape(1, width)
    for c in act_copies():
        c.wait()
    normalize(x_scr, vec_scr, x_scr)

    @pl.loop(0, n_pairs)
    def _(i):
        @pl.when((i > 0) & (i < n_pairs - 1))
        def _():
            mem_copy(i - 1).start()

        for c in weight_copies(i):
            c.wait()
        block, r = wo_rows(i)
        q = (dot(x_scr[...], m_scr[wq_at:wo_at, :, cols(i)].reshape(width, PAIR), NN) + pair_of(vec_scr, 2, i)).astype(BF16)
        d = dot(gy_scr[...], m_scr[wo_at + block, r, :], NT).astype(BF16)
        q2, d2 = split_heads(q.astype(F32), n_seq), split_heads(d.astype(F32), n_seq)
        q2_scr[i] = q2
        d2_scr[i] = d2
        place(zg_scr, 0, i, q2, lambda j, step: wk_scr[j:j + step, cols(i)])
        place(zg_scr, 1, i, d2, lambda j, step: wv_scr[j:j + step, cols(i)])
        ps_scr[i] = dot(d2, jnp.broadcast_to(pair_of(vec_scr, 3, i).astype(BF16), (PAIR, PAIR)), NT)

    for g in (n_pairs - 2, n_pairs - 1):
        mem_copy(g).start()
    for c in q_copies():
        c.start()

    @pl.loop(0, n_pairs)
    def _(g):
        mem_copy(g).wait()
        for j in range(n_blk):
            b = g * n_blk + j
            at = pl.ds(b, 1)
            t = dot(m_scr[b], zg_scr[:, :, seq_rows(b), :].reshape(2 * rows, width), NT)
            s = t[:, :rows] * scale
            dp = t[:, rows:] + ps_scr[:, seq_rows(b), :].reshape(rows, PAIR).T[0:1, :]
            mx = jnp.max(s, axis=0, keepdims=True)
            e = jnp.exp(s - mx)
            e_scr[g, j * n_fr:(j + 1) * n_fr, :] = e
            dp_scr[g, j * n_fr:(j + 1) * n_fr, :] = dp
            st_scr[0, at, :] = mx
            st_scr[1, at, :] = jnp.sum(e, axis=0, keepdims=True)
            st_scr[2, at, :] = jnp.sum(e * dp, axis=0, keepdims=True)

    pl.semaphore_wait(barrier, n_cp - 1)
    for k in range(n_cp - 1):
        stats_copy(k).start()
    for k in range(n_cp - 1):
        stats_copy(k).wait()

    @pl.loop(0, n_pairs)
    def _(g):
        @pl.when(g >= 2)
        def _():
            pg_copy(g - 2).wait()

        slot = lax.rem(g, 2)
        ones = jnp.ones((n_fr, PAIR), BF16)
        for j in range(n_blk):
            b = g * n_blk + j
            at = pl.ds(b, 1)
            tops = [st_scr[0, at, :]] + [other[k, 0, at, :] for k in range(n_cp - 1)]
            sums_l = [st_scr[1, at, :]] + [other[k, 1, at, :] for k in range(n_cp - 1)]
            sums_c = [st_scr[2, at, :]] + [other[k, 2, at, :] for k in range(n_cp - 1)]
            top = functools.reduce(jnp.maximum, tops)
            fac = [jnp.exp(t - top) for t in tops]
            total = functools.reduce(jnp.add, [f * v for f, v in zip(fac, sums_l)])
            c = functools.reduce(jnp.add, [f * v for f, v in zip(fac, sums_c)]) / total
            p = e_scr[g, j * n_fr:(j + 1) * n_fr, :] * (fac[0] / total)
            gr = p * (dp_scr[g, j * n_fr:(j + 1) * n_fr, :] - c) * scale
            pg = jnp.concatenate([gr.astype(BF16), p.astype(BF16)], axis=1)
            pg_scr[slot, j] = pg
            pgt = pg.T
            step = 256
            for w in range(0, width, step):
                t = dot(pgt, m_scr[b, :, w:w + step], NN).astype(BF16)
                zg_scr[:, :, seq_rows(b), w:w + step] = t.reshape(2, n_pairs, n_row, step)
            ps_scr[:, seq_rows(b), :] = dot(pgt[rows:], ones, NN).reshape(n_pairs, n_row, PAIR)
        pg_copy(g).start()

    def o_and_dq(k):
        o = join_heads(dot(zg_scr[1, k], wv_scr[:, cols(k)], NN), n_seq) + join_heads(ps_scr[k], n_seq) * pair_of(vec_scr, 3, k)
        dq = join_heads(dot(zg_scr[0, k], wk_scr[:, cols(k)], NN), n_seq)
        for part, t in enumerate((o, dq)):
            top, bottom = t[:t.shape[0] // 2], t[t.shape[0] // 2:]
            mine_oq[k, part] = jnp.where(first, top, bottom)
            theirs_oq[k, part] = jnp.where(first, bottom, top)

    @pl.loop(0, n_pairs // 2)
    def _(k):
        o_and_dq(k)

    oq_mate(0).start()

    @pl.loop(n_pairs // 2, n_pairs)
    def _(k):
        o_and_dq(k)

    oq_mate(1).start()
    add_mate(0)
    oq_across(0).start()

    def close_dw(k):
        dw_mate(k).wait()
        e_scr[k] += got_dw[k]

    @pl.loop(0, n_pairs)
    def _(k):
        @pl.when(k >= 1)
        def _():
            dw_mate(k - 1).start()

        @pl.when(k == 3)
        def _():
            oq_across(1).start()

        @pl.when(k >= 5)
        def _():
            for c in chip_copies(k - 5):
                c.start()

        small_scr[me, 1, pl.ds(k, 1), :] = jnp.sum(ps_scr[k] * d2_scr[k].astype(F32), axis=0, keepdims=True)
        dwk = dot(zg_scr[0, k], q2_scr[k], TN)
        dwv = dot(zg_scr[1, k], d2_scr[k], TN)
        e_scr[k] = jnp.where(first, dwk, dwv)
        dp_scr[k] = jnp.where(first, dwv, dwk)

        @pl.when(k == 2)
        def _():
            add_mate(1)

        @pl.when(k >= 4)
        def _():
            close_dw(k - 4)

    dw_mate(n_pairs - 1).start()

    @pl.loop(n_pairs - 4, n_pairs)
    def _(k):
        close_dw(k)

    @pl.loop(n_pairs - 5, n_pairs)
    def _(k):
        for c in chip_copies(k):
            c.start()

    finish(0)
    own_across(0).start()
    finish(1)
    own_across(1).start()
    for k in range(n_cp - 1):
        small_copy(k).start()
    own_across(0).wait()
    half_mate(0).start()
    own_across(1).wait()
    half_mate(1).start()
    for k in range(n_cp - 1):
        small_copy(k).wait()
    small_ref[...] = small_scr[0] + small_scr[1] + small_scr[2] + small_scr[3]
    half_mate(0).wait()
    half_mate(1).wait()
    for c in out_copies():
        c.start()

    @pl.loop(0, n_pairs)
    def _(k):
        for c in chip_copies(k):
            c.wait()

    for g in (n_pairs - 2, n_pairs - 1):
        pg_copy(g).wait()
    for c in q_copies() + out_copies():
        c.wait()


def assemble_kernel(core_ref, fin_ref, other_ref, *refs):
    wk_ref, wv_ref = refs[-2:]
    first = core_ref[0] == 0
    wk_ref[...] = jnp.where(first, fin_ref[...], other_ref[...])
    wv_ref[...] = jnp.where(first, other_ref[...], fin_ref[...])


def assemble(core, fin, other, at, acc):
    n, width = fin.shape
    step = 192 if n % 192 == 0 and at % 192 == 0 else 64
    block = pl.BlockSpec((step, width), lambda i: (i, 0))
    out = pl.BlockSpec((step, width), lambda i: (at // step + i, 0))
    return pl.pallas_call(
        assemble_kernel, grid=(n // step,), name="assemble",
        in_specs=[pl.BlockSpec(memory_space=pltpu.SMEM), block, block] + [pl.BlockSpec(memory_space=pl.ANY)] * len(acc),
        out_specs=[out, out], out_shape=[jax.ShapeDtypeStruct((width, width), F32)] * 2,
        input_output_aliases={3: 0, 4: 1} if acc else {},
        compiler_params=pltpu.CompilerParams(dimension_semantics=("arbitrary",)),
    )(core, fin, other, *acc)


def mem_kernel(n_first, q2_ref, d2_ref, wk_ref, wv_ref, pg_ref, dm_ref, z_scr):
    i = pl.program_id(0)
    _, n_pairs, _, width = z_scr.shape
    n_blk = pg_ref.shape[0]
    n_row = pg_ref.shape[2] // (2 * n_pairs)

    @pl.when(i < n_first)
    def _():
        place(z_scr, 0, i, q2_ref[0], lambda j, step: wk_ref[j:j + step, :])
        place(z_scr, 1, i, d2_ref[0], lambda j, step: wv_ref[j:j + step, :])

    @pl.when(i >= n_first)
    def _():
        for j in range(n_blk):
            b = (i - n_first) * n_blk + j
            at = pl.ds(pl.multiple_of(b * n_row, n_row), n_row)
            z = z_scr[:, :, at, :].reshape(pg_ref.shape[2], width)
            dm_ref[j] = dot(pg_ref[j], z, NN).astype(BF16)


def params():
    return pltpu.CompilerParams(dimension_semantics=("arbitrary",), vmem_limit_bytes=VMEM_LIMIT)


def solution(mesh):
    act_spec = P("dp", None, None)
    mem_spec = P("dp", "cp", None)
    vec_out = P("dp")
    mat_out = P("dp", None)
    in_specs = (act_spec, mem_spec, P(), P(), P(), P(), P(), P(), P(), P(), P(), act_spec)
    out_specs = (act_spec, act_spec, mem_spec, vec_out, vec_out, mat_out, vec_out, mat_out, mat_out, vec_out, mat_out, vec_out)
    n_cp = mesh.shape["cp"]

    def swap(x, bit):
        return lax.ppermute(x, "cp", [(i, i ^ bit) for i in range(n_cp)])

    def device_step(hidden, memory, ln_gain, ln_bias, w_q, b_q, w_k, w_v, b_v, w_o, b_o, grad_y):
        n_seq, n_tok, width = hidden.shape
        n_fr = memory.shape[1]
        n_heads = width // HEAD
        n_pairs = n_heads // 2
        rows = n_heads * n_tok
        tokens = n_seq * n_tok
        scale = HEAD ** -0.5
        core = lax.axis_index("cp") % 2
        h2, gy2 = hidden.reshape(tokens, width), grad_y.reshape(tokens, width)
        blk = n_seq // n_pairs
        quarter = tokens // 4
        chunks = [width * 3 // 8, width * 3 // 8, width * 3 // 16, width // 16]
        anywhere = pl.BlockSpec(memory_space=pl.ANY)
        vm = lambda dt, *s: pltpu.VMEM(s, dt)
        sems = lambda *n: pltpu.SemaphoreType.DMA(n)
        both = lambda n: [sems(n)] * 2
        pg, *rest = pl.pallas_call(
            functools.partial(fused_kernel, scale, n_cp), name="fused",
            in_specs=[anywhere] * 7 + [pl.BlockSpec(memory_space=pltpu.VMEM)] * 4,
            out_specs=[anywhere] * 8 + [pl.BlockSpec(memory_space=pltpu.VMEM)],
            out_shape=[jax.ShapeDtypeStruct((n_seq, n_fr, 2 * rows), BF16)]
            + [jax.ShapeDtypeStruct((c, width), F32) for c in chunks]
            + [jax.ShapeDtypeStruct((2, tokens, width), BF16)]
            + [jax.ShapeDtypeStruct((n_pairs, 2 * tokens, PAIR), BF16)] * 2
            + [jax.ShapeDtypeStruct((2, n_pairs, PAIR), F32)],
            scratch_shapes=[vm(BF16, tokens, width), vm(BF16, tokens, width), vm(F32, 4, width),
                            vm(BF16, 2, n_pairs, 2 * tokens, width), vm(BF16, n_seq, n_fr, width),
                            vm(F32, n_pairs, blk * n_fr, rows), vm(F32, n_pairs, blk * n_fr, rows),
                            vm(BF16, width, width), vm(BF16, width, width), vm(F32, n_pairs, 2 * tokens, PAIR),
                            vm(BF16, n_pairs, 2 * tokens, PAIR), vm(BF16, n_pairs, 2 * tokens, PAIR),
                            vm(F32, 3, n_seq, rows), vm(F32, n_cp - 1, 3, n_seq, rows),
                            vm(F32, n_pairs, 2, 2 * quarter, PAIR), vm(F32, n_pairs, 2, 2 * quarter, PAIR),
                            vm(F32, n_pairs, 2, 2 * quarter, PAIR), vm(F32, n_pairs, 2, quarter, PAIR),
                            vm(F32, n_pairs, 2, quarter, PAIR), vm(F32, n_pairs, 2, quarter, PAIR),
                            vm(BF16, n_pairs, 2, tokens, PAIR), vm(F32, n_cp, 2, n_pairs, PAIR),
                            vm(F32, n_pairs, width, PAIR),
                            sems(2), sems(4, n_pairs), sems(n_pairs), sems(2), sems(4, n_pairs), sems(2, n_pairs),
                            sems(2), vm(BF16, 2, blk, n_fr, 2 * rows)]
            + both(n_cp - 1) + both(2) + both(2) + both(2) + both(2) + both(n_pairs) + both(n_cp - 1),
            compiler_params=pltpu.CompilerParams(vmem_limit_bytes=VMEM_LIMIT, collective_id=0, has_side_effects=True),
        )(h2, gy2, w_q.reshape(blk, n_fr, width), w_k, w_v, w_o.reshape(blk, n_fr, width), memory, ln_gain, ln_bias, b_q, b_v)
        chips, (oq, q2, d2, small) = rest[:4], rest[4:]
        attn_out, dq_low = oq[0], oq[1]
        small = small.reshape(2, width)
        grad_bq, grad_bv = small[0], small[1]

        got = []
        for c in chips:
            got.append(swap(c, 2))

        hidden_f32 = h2.astype(F32)
        centered = hidden_f32 - jnp.mean(hidden_f32, axis=-1, keepdims=True)
        inv_std = lax.rsqrt(jnp.mean(centered * centered, axis=-1, keepdims=True) + EPS)
        x_hat = centered * inv_std
        gain_f32 = ln_gain.astype(F32)
        x_norm = (x_hat * gain_f32 + ln_bias.astype(F32)).astype(BF16)
        out_y = (hidden_f32 + dot(attn_out, w_o, NN) + b_o.astype(F32)).astype(BF16)
        grad_wo = dot(attn_out, gy2, TN)
        grad_bo = jnp.sum(gy2, axis=0, dtype=F32)
        grad_wq = dot(x_norm, dq_low, TN)
        d_xnorm = dot(dq_low, w_q, NT)
        grad_ln_gain = jnp.sum(d_xnorm * x_hat, axis=0)
        grad_ln_bias = jnp.sum(d_xnorm, axis=0)
        d_hat = d_xnorm * gain_f32
        d_hidden = inv_std * (d_hat - jnp.mean(d_hat, axis=-1, keepdims=True) - x_hat * jnp.mean(d_hat * x_hat, axis=-1, keepdims=True))
        grad_h = (gy2.astype(F32) + d_hidden).astype(BF16)

        pair_block = pl.BlockSpec((1, 2 * tokens, PAIR), lambda i: (jnp.minimum(i, n_pairs - 1), 0, 0))
        col_block = pl.BlockSpec((width, PAIR), lambda i: (0, jnp.minimum(i, n_pairs - 1)))
        late = lambda *s: pl.BlockSpec((blk,) + s, lambda i: (jnp.maximum(i - n_pairs, 0), 0, 0))
        grad_mem = pl.pallas_call(
            functools.partial(mem_kernel, n_pairs), grid=(2 * n_pairs,), name="mem",
            in_specs=[pair_block, pair_block, col_block, col_block, late(n_fr, 2 * rows)], out_specs=late(n_fr, width),
            out_shape=jax.ShapeDtypeStruct((n_seq, n_fr, width), BF16), compiler_params=params(),
            scratch_shapes=[vm(BF16, 2, n_pairs, 2 * tokens, width)],
            cost_estimate=pl.CostEstimate(flops=8 * n_seq * n_fr * rows * width, bytes_accessed=40 << 20, transcendentals=0),
        )(q2, d2, w_k, w_v, pg)

        hidden_work = (out_y, grad_h, grad_mem, grad_ln_gain, grad_ln_bias, grad_wq, grad_wo, grad_bo)
        got[0], hidden_work = lax.optimization_barrier((got[0], hidden_work))
        out_y, grad_h, grad_mem, grad_ln_gain, grad_ln_bias, grad_wq, grad_wo, grad_bo = hidden_work
        core_arr = core.reshape(1).astype(jnp.int32)
        acc, at = (), 0
        for c, g in zip(chips, got):
            g, acc = lax.optimization_barrier((g, acc))
            fin = c + g
            acc = assemble(core_arr, fin, swap(fin, 1), at, acc)
            at += c.shape[0]
        grad_wk, grad_wv = acc
        return (out_y.reshape(hidden.shape), grad_h.reshape(hidden.shape), grad_mem, grad_ln_gain, grad_ln_bias,
                grad_wq, grad_bq, grad_wk, grad_wv, grad_bv, grad_wo, grad_bo)

    return jax.shard_map(device_step, mesh=mesh, in_specs=in_specs, out_specs=out_specs, check_vma=False)
```

profile of v0, /device:TPU:0, one launch (start us, length us, event | category | flops | bytes accessed | tf_op | source)
XLA Modules:
  0.0 172.2 jit_solution(2383399631227979719)
XLA Ops:
  0.6 58.3 %fused.1 = (bf16[32,256,256]{2,1,0:T(8,128)(2,1)}, f32[384,1024]{1,0:T(8,128)}, f32[384,1024]{1,0:T(8,128)}, f32[192,1024]{1,0:T(8,128)}, f32[64,1024]{1,0:T(8,1...) custom-call(bf16[256,1024]{1,0:T(8,128)(2,1)} %bitcast.35, ...), custom_call_target="tpu_custom_call" | custom-call | tf_op jit(solution)/shard_map/fused/pallas_call | solution.py:429
  59.0 2.2 %collective-permute-start = (f32[384,1024]{1,0:T(8,128)}, f32[384,1024]{1,0:T(8,128)}, u32[]{:S(2)}, u32[]{:S(2)}) collective-permute-start(f32[384,1024]{1,0:T(8,128)} %get-tuple-element.47), channel_id=1, source_target_pairs={{0,2},{1,3},{2,0},{3,1},{4,6},{5,7},{6,4},{7,5},{8,10},{9,11},{10,... | collective-permute-start | bytes 4718600 | tf_op jit(solution)/shard_map/ppermute | solution.py:410
  61.2 1.2 convert_reduce_fusion
  62.4 1.3 fusion.4
  63.7 0.1 div.17
  63.8 0.7 convert_element_type.41
  64.5 0.1 rsqrt.13
  64.6 0.7 convert_element_type.37
  65.2 0.0 copy-start
  65.2 0.0 copy-start.5
  65.2 0.0 copy-start.6
  65.3 3.5 %fusion.1 = bf16[256,1024]{1,0:T(8,128)(2,1)} fusion(bf16[1024,1024]{1,0:T(8,128)(2,1)} %param.21, f32[1024]{0:T(1024)S(1)} %convert_element_type.37, bf16[2,256,1024]{2,1,0:T(8,128)(2,1)} %get-tuple-element.48, bf16[32,8,1024]{2,1,0:T(8,128)(2,1)} %param.12), kind=kOutput, calls=%fused_computation.5 | convolution fusion | flops 537919488 | bytes 3674112 | tf_op jit(solution)/shard_map/dot_general | solution.py:23
  68.7 0.0 copy-done
  68.8 0.0 copy-done.5
  68.8 0.0 copy-done.6
  68.8 0.0 copy-start.1
  68.8 1.6 fusion.17
  70.3 0.0 copy-start.13
  70.3 0.0 copy-done.1
  70.3 1.2 fusion.16
  71.6 0.7 convert_reduce_fusion.1
  72.3 0.0 copy-done.13
  72.3 2.8 %fusion.24 = f32[1024,1024]{1,0:T(8,128)} fusion(bf16[2,256,1024]{2,1,0:T(8,128)(2,1)S(1)} %copy-done.6, bf16[32,8,1024]{2,1,0:T(8,128)(2,1)S(1)} %copy-done.1), kind=kOutput, calls=%fused_computation.29 | convolution fusion | flops 536870912 | bytes 5242880 | tf_op jit(solution)/shard_map/dot_general | solution.py:23
  75.0 2.9 %fusion.19 = f32[1024,1024]{1,0:T(8,128)} fusion(bf16[32,8,1024]{2,1,0:T(8,128)(2,1)S(1)} %copy-done, f32[1024]{0:T(1024)S(1)} %convert_element_type.43, f32[1024]{0:T(1024)S(1)} %convert_element_type.41, f32[32,8]{1,0:T(8,128)S(1)} %add_rsqrt_fusion, f32[32,8]{1,0:T(8,128)S(1)} %broadcast_multiply_fusion, bf16[2,256,1024]{2,1,0:T(8,128)(2,1)S(1)} %copy-done.6), kind=kOutput, calls=%fused_computation.25 | convolution fusion | flops 538443776 | bytes 5283840 | tf_op jit(solution)/shard_map/dot_general | solution.py:23
  78.0 18.6 %mem.1 = bf16[32,256,1024]{2,1,0:T(8,128)(2,1)} custom-call(bf16[8,512,128]{2,1,0:T(8,128)(2,1)} %get-tuple-element.49.q2_ref, bf16[8,512,128]{2,1,0:T(8,128)(2,1)} %get-tuple-element.50.d2_ref, bf16[1024,1024]{1,0:T(8,128)(2,1)} %wk_ref.3, bf16[1024,1024]{1,0:T(8,128)(2,1)} %wv_ref.3, bf16[32,256,256]{2,1,0:T(8,128)(2,1)} %get-tuple-element.51.pg_ref), custom_call_target="tpu_custom_call" | custom-call | flops 8589934592 | bytes 41943040 | tf_op jit(solution)/shard_map/mem/pallas_call | solution.py:483
  96.6 0.0 collective-permute-done
  96.6 0.0 copy-start.7
  96.6 2.3 %add.61.fin_ref = f32[384,1024]{1,0:T(8,128)S(1)} add(f32[384,1024]{1,0:T(8,128)} %get-tuple-element.47, f32[384,1024]{1,0:T(8,128)} %collective-permute-done) | non-fusion elementwise | flops 393216 | bytes 4718592 | tf_op jit(solution)/shard_map/add | solution.py:498
  98.9 0.0 copy-start.2
  98.9 0.1 collective-permute-start.4
  99.0 0.0 copy-done.7
  99.0 1.5 collective-permute-start.3
  100.5 1.9 %collective-permute-done.4.other_ref = f32[384,1024]{1,0:T(8,128)} collective-permute-done((f32[384,1024]{1,0:T(8,128)S(1)}, f32[384,1024]{1,0:T(8,128)}, u32[]{:S(2)}, u32[]{:S(2)}) %collective-permute-start.4) | collective-permute-done | bytes 1572896 | tf_op jit(solution)/shard_map/ppermute | solution.py:410
  102.4 0.0 copy-done.2
  102.4 3.2 %assemble.4 = (f32[1024,1024]{1,0:T(8,128)}, f32[1024,1024]{1,0:T(8,128)}) custom-call(s32[1]{0:T(128)} %bitcast.10.core_ref, f32[384,1024]{1,0:T(8,128)} %copy-done.2, f32[384,1024]{1,0:T(8,128)} %collective-permute-done.4.other_ref), custom_call_target="tpu_custom_call" | custom-call | tf_op jit(solution)/shard_map/assemble/pallas_call | solution.py:367
  105.6 30.2 %collective-permute-done.3 = f32[384,1024]{1,0:T(8,128)} collective-permute-done((f32[384,1024]{1,0:T(8,128)S(1)}, f32[384,1024]{1,0:T(8,128)}, u32[]{:S(2)}, u32[]{:S(2)}) %collective-permute-start.3) | collective-permute-done | bytes 1572896 | tf_op jit(solution)/shard_map/ppermute | solution.py:410
  135.8 1.7 add.62.fin_ref
  137.5 0.0 copy-start.3
  137.5 0.0 collective-permute-start.5
  137.5 1.6 collective-permute-start.2
  139.1 1.8 %collective-permute-done.5.other_ref = f32[384,1024]{1,0:T(8,128)S(1)} collective-permute-done((f32[384,1024]{1,0:T(8,128)S(1)}, f32[384,1024]{1,0:T(8,128)S(1)}, u32[]{:S(2)}, u32[]{:S(2)}) %collective-permute-start.5) | collective-permute-done | bytes 1572896 | tf_op jit(solution)/shard_map/ppermute | solution.py:410
  140.9 0.0 copy-done.3
  141.0 1.2 copy-done.8
  142.1 3.2 %assemble.5 = (f32[1024,1024]{1,0:T(8,128)}, f32[1024,1024]{1,0:T(8,128)}) custom-call(s32[1]{0:T(128)} %bitcast.10.core_ref, f32[384,1024]{1,0:T(8,128)} %copy-done.3, f32[384,1024]{1,0:T(8,128)} %copy-done.8, f32[1024,1024]{1,0:T(8,128)} %get-tuple-element.66.refs_0_, ...), custom_call_target="tpu_custom_call", output_to_operand_aliasing={{0}: (3, {}), {1}: (4, {})} | custom-call | tf_op jit(solution)/shard_map/assemble/pallas_call | solution.py:367
  145.3 12.5 %collective-permute-done.2 = f32[192,1024]{1,0:T(8,128)} collective-permute-done((f32[192,1024]{1,0:T(8,128)}, f32[192,1024]{1,0:T(8,128)}, u32[]{:S(2)}, u32[]{:S(2)}) %collective-permute-start.2) | collective-permute-done | bytes 786464 | tf_op jit(solution)/shard_map/ppermute | solution.py:410
  157.8 1.5 add.63.fin_ref
  159.3 0.0 copy-start.4
  159.3 0.0 collective-permute-start.6
  159.3 0.0 copy-done.11
  159.3 0.0 copy-start.14
  159.4 1.6 collective-permute-start.1
  160.9 0.7 collective-permute-done.6.other_ref
  161.6 0.0 copy-done.4
  161.6 0.9 copy-done.10
  162.5 2.6 %assemble.6 = (f32[1024,1024]{1,0:T(8,128)}, f32[1024,1024]{1,0:T(8,128)}) custom-call(s32[1]{0:T(128)} %bitcast.10.core_ref, f32[192,1024]{1,0:T(8,128)} %copy-done.4, f32[192,1024]{1,0:T(8,128)} %copy-done.10, f32[1024,1024]{1,0:T(8,128)} %get-tuple-element.71.refs_0_, ...), custom_call_target="tpu_custom_call", output_to_operand_aliasing={{0}: (3, {}), {1}: (4, {})} | custom-call | tf_op jit(solution)/shard_map/assemble/pallas_call | solution.py:367
  165.1 2.9 %collective-permute-done.1 = f32[64,1024]{1,0:T(8,128)S(1)} collective-permute-done((f32[64,1024]{1,0:T(8,128)S(1)}, f32[64,1024]{1,0:T(8,128)S(1)}, u32[]{:S(2)}, u32[]{:S(2)}) %collective-permute-start.1) | collective-permute-done | bytes 262176 | tf_op jit(solution)/shard_map/ppermute | solution.py:410
  168.1 0.0 copy-start.9
  168.1 0.0 collective-permute-start.7
  168.1 0.0 copy-done.14
  168.1 0.6 slice_bitcast_fusion
  168.8 0.9 collective-permute-done.7.other_ref
  169.7 0.0 copy-done.9
  169.7 0.7 copy-done.12
  170.4 1.9 %assemble.7 = (f32[1024,1024]{1,0:T(8,128)}, f32[1024,1024]{1,0:T(8,128)}) custom-call(s32[1]{0:T(128)} %bitcast.10.core_ref, f32[64,1024]{1,0:T(8,128)} %copy-done.9, f32[64,1024]{1,0:T(8,128)} %copy-done.12, f32[1024,1024]{1,0:T(8,128)} %get-tuple-element.76.refs_0_, ...), custom_call_target="tpu_custom_call", output_to_operand_aliasing={{0}: (3, {}), {1}: (4, {})} | custom-call | tf_op jit(solution)/shard_map/assemble/pallas_call | solution.py:367
  (9 shorter events, 0.1 us)
Async XLA Ops:
  59.0 37.6 %collective-permute-start = (f32[384,1024]{1,0:T(8,128)}, f32[384,1024]{1,0:T(8,128)}, u32[]{:S(2)}, u32[]{:S(2)}) collective-permute-start(f32[384,1024]{1,0:T(8,128)} %get-tuple-element.47), channel_id=1, source_target_pairs={{0,2},{1,3},{2,0},{3,1},{4,6},{5,7},{6,4},{7,5},{8,10},{9,11},{10,... | collective-permute-start | bytes 4718600 | tf_op jit(solution)/shard_map/ppermute | solution.py:410
  65.2 3.5 %copy-start = (bf16[32,8,1024]{2,1,0:T(8,128)(2,1)S(1)}, bf16[32,8,1024]{2,1,0:T(8,128)(2,1)}, u32[]{:S(2)}) copy-start(bf16[32,8,1024]{2,1,0:T(8,128)(2,1)} %param.12) | copy-start | bytes 1572868
  65.2 3.5 %copy-start.5 = (bf16[1024,1024]{1,0:T(8,128)(2,1)S(1)}, bf16[1024,1024]{1,0:T(8,128)(2,1)}, u32[]{:S(2)}) copy-start(bf16[1024,1024]{1,0:T(8,128)(2,1)} %param.16) | copy-start | bytes 6291460
  65.2 3.5 %copy-start.6 = (bf16[2,256,1024]{2,1,0:T(8,128)(2,1)S(1)}, bf16[2,256,1024]{2,1,0:T(8,128)(2,1)}, u32[]{:S(2)}) copy-start(bf16[2,256,1024]{2,1,0:T(8,128)(2,1)} %get-tuple-element.48) | copy-start | bytes 3145732
  68.8 1.6 copy-start.1
  70.3 1.9 %copy-start.13 = (bf16[1024]{0:T(1024)(128)(2,1)S(1)}, bf16[1024]{0:T(1024)(128)(2,1)}, u32[]{:S(2)}) copy-start(bf16[1024]{0:T(1024)(128)(2,1)} %bias_ref.1) | copy-start | bytes 6148
  96.6 2.4 %copy-start.7 = (f32[384,1024]{1,0:T(8,128)S(1)}, f32[384,1024]{1,0:T(8,128)}, u32[]{:S(2)}) copy-start(f32[384,1024]{1,0:T(8,128)} %get-tuple-element.61) | copy-start | bytes 4718596
  98.9 3.6 %copy-start.2 = (f32[384,1024]{1,0:T(8,128)}, f32[384,1024]{1,0:T(8,128)S(1)}, u32[]{:S(2)}) copy-start(f32[384,1024]{1,0:T(8,128)S(1)} %add.61.fin_ref) | copy-start | bytes 4718596
  98.9 3.6 %collective-permute-start.4 = (f32[384,1024]{1,0:T(8,128)S(1)}, f32[384,1024]{1,0:T(8,128)}, u32[]{:S(2)}, u32[]{:S(2)}) collective-permute-start(f32[384,1024]{1,0:T(8,128)S(1)} %add.61.fin_ref), channel_id=1, source_target_pairs={{0,1},{1,0},{2,3},{3,2},{4,5},{5,4},{6,7},{7,6},{8,9},{9,8},{10,11... | collective-permute-start | bytes 4718600 | tf_op jit(solution)/shard_map/ppermute | solution.py:410
  99.0 36.8 %collective-permute-start.3 = (f32[384,1024]{1,0:T(8,128)S(1)}, f32[384,1024]{1,0:T(8,128)}, u32[]{:S(2)}, u32[]{:S(2)}) collective-permute-start(f32[384,1024]{1,0:T(8,128)S(1)} %copy-done.7), channel_id=1, source_target_pairs={{0,2},{1,3},{2,0},{3,1},{4,6},{5,7},{6,4},{7,5},{8,10},{9,11},{10,... | collective-permute-start | bytes 4718600 | tf_op jit(solution)/shard_map/ppermute | solution.py:410
  137.5 3.5 %copy-start.3 = (f32[384,1024]{1,0:T(8,128)}, f32[384,1024]{1,0:T(8,128)S(1)}, u32[]{:S(2)}) copy-start(f32[384,1024]{1,0:T(8,128)S(1)} %add.62.fin_ref) | copy-start | bytes 4718596
  137.5 3.4 %collective-permute-start.5 = (f32[384,1024]{1,0:T(8,128)S(1)}, f32[384,1024]{1,0:T(8,128)S(1)}, u32[]{:S(2)}, u32[]{:S(2)}) collective-permute-start(f32[384,1024]{1,0:T(8,128)S(1)} %add.62.fin_ref), channel_id=1, source_target_pairs={{0,1},{1,0},{2,3},{3,2},{4,5},{5,4},{6,7},{7,6},{8,9},{9,8},{10,11... | collective-permute-start | bytes 4718600 | tf_op jit(solution)/shard_map/ppermute | solution.py:410
  137.5 20.3 %collective-permute-start.2 = (f32[192,1024]{1,0:T(8,128)}, f32[192,1024]{1,0:T(8,128)}, u32[]{:S(2)}, u32[]{:S(2)}) collective-permute-start(f32[192,1024]{1,0:T(8,128)} %get-tuple-element.60), channel_id=1, source_target_pairs={{0,2},{1,3},{2,0},{3,1},{4,6},{5,7},{6,4},{7,5},{8,10},{9,11},{10,... | collective-permute-start | bytes 2359304 | tf_op jit(solution)/shard_map/ppermute | solution.py:410
  140.9 1.2 copy-start.8
  145.3 14.0 %copy-start.11 = (f32[64,1024]{1,0:T(8,128)S(1)}, f32[64,1024]{1,0:T(8,128)}, u32[]{:S(2)}) copy-start(f32[64,1024]{1,0:T(8,128)} %get-tuple-element.59) | copy-start | bytes 786436
  159.3 2.3 %copy-start.4 = (f32[192,1024]{1,0:T(8,128)}, f32[192,1024]{1,0:T(8,128)S(1)}, u32[]{:S(2)}) copy-start(f32[192,1024]{1,0:T(8,128)S(1)} %add.63.fin_ref) | copy-start | bytes 2359300
  159.3 2.3 %collective-permute-start.6 = (f32[192,1024]{1,0:T(8,128)S(1)}, f32[192,1024]{1,0:T(8,128)S(1)}, u32[]{:S(2)}, u32[]{:S(2)}) collective-permute-start(f32[192,1024]{1,0:T(8,128)S(1)} %add.63.fin_ref), channel_id=1, source_target_pairs={{0,1},{1,0},{2,3},{3,2},{4,5},{5,4},{6,7},{7,6},{8,9},{9,8},{10,11... | collective-permute-start | bytes 2359304 | tf_op jit(solution)/shard_map/ppermute | solution.py:410
  159.3 8.8 %copy-start.14 = (f32[2,8,128]{2,1,0:T(8,128)S(1)}, f32[2,8,128]{2,1,0:T(8,128)}, u32[]{:S(2)}) copy-start(f32[2,8,128]{2,1,0:T(8,128)} %get-tuple-element.58) | copy-start | bytes 24580
  159.4 8.7 %collective-permute-start.1 = (f32[64,1024]{1,0:T(8,128)S(1)}, f32[64,1024]{1,0:T(8,128)S(1)}, u32[]{:S(2)}, u32[]{:S(2)}) collective-permute-start(f32[64,1024]{1,0:T(8,128)S(1)} %copy-done.11), channel_id=1, source_target_pairs={{0,2},{1,3},{2,0},{3,1},{4,6},{5,7},{6,4},{7,5},{8,10},{9,11},{10,... | collective-permute-start | bytes 786440 | tf_op jit(solution)/shard_map/ppermute | solution.py:410
  161.6 0.9 copy-start.10
  168.1 1.6 copy-start.9
  168.1 1.6 collective-permute-start.7
  169.7 0.7 copy-start.12
where the time goes:
time: 173 us; the launch traced here: 172 us
  Pallas kernels  87.8 us (51%)
  waiting for transfers between devices  50.9 us (29%)
  other arithmetic  11.3 us (7%)
  matrix products  10.7 us (6%)
  starting transfers between devices  7.15 us (4%)
  local copies, waits for them, and re-layouts  3.62 us (2%)
    pallas_call x1, Pallas kernels, device_step(): pl.pallas_call(functools.partial(fused_kernel, scale, n_cp), name='fused'...  58.3 us
    ppermute x8, waiting for transfers between devices, swap(): return lax.ppermute(x, 'cp', [(i, i ^ bit) for i in range(n_cp)])  50.9 us
    pallas_call x1, Pallas kernels, device_step(): pl.pallas_call(functools.partial(mem_kernel, n_pairs), grid=(2 * n_pairs,...  18.6 us
    pallas_call x4, Pallas kernels, assemble(): pl.pallas_call(assemble_kernel, grid=(n // step,), name='assemble', in_sp...  10.8 us
    dot_general x4, matrix products, dot(): return lax.dot_general(a, b, dims, preferred_element_type=F32)  10.7 us
    ppermute x8, starting transfers between devices, swap(): return lax.ppermute(x, 'cp', [(i, i ^ bit) for i in range(n_cp)])  7.15 us
    add x4, other arithmetic, device_step(): fin = c + g  5.42 us
  transfers between devices with their start and end apart: 8, of which 7 were waited for; matrix products, arithmetic and copies ran while one was open for 10% of the time, Pallas kernels for 16%

commit v1 on v0

--- a/solution.py
+++ b/solution.py
@@ -62,18 +62,22 @@
 
 
 def fused_kernel(scale, n_cp, h_ref, gy_ref, wq_ref, wk_ref, wv_ref, wo_ref, m_ref, gain_ref, bias_ref, bq_ref, bv_ref,
-                 pg_ref, chip0_ref, chip1_ref, chip2_ref, chip3_ref, oq_ref, q2_out, d2_out, small_ref,
+                 pg_ref, chip0_ref, chip1_ref, chip2_ref, chip3_ref, head_ref, head_got, oq_ref, q2_out, d2_out, small_ref,
                  x_scr, gy_scr, vec_scr, zg_scr, m_scr, e_scr, dp_scr, wk_scr, wv_scr, ps_scr, q2_scr, d2_scr, st_scr, other,
                  mine_oq, theirs_oq, got_oq, keep_x, give_x, got_x, full_oq, small_scr, got_dw,
-                 in_sem, w_sem, m_sem, q_sem, chip_sem, out_sem, pg_sem, pg_scr,
-                 st_s, st_r, rd_s, rd_r, rx_s, rx_r, ax_s, ax_r, ad_s, ad_r, dw_s, dw_r, sm_s, sm_r):
+                 in_sem, w_sem, m_sem, q_sem, chip_sem, head_sem, out_sem, pg_sem, pg_scr,
+                 st_s, st_r, rd_s, rd_r, rx_s, rx_r, ax_s, ax_r, ad_s, ad_r, dw_s, dw_r, sm_s, sm_r, xd_s, xd_r):
     _, n_pairs, n_rows, width = zg_scr.shape
     n_seq, n_fr, _ = m_scr.shape
     n_row = n_rows // n_seq
     rows = n_row * n_pairs
     n_blk = n_seq // n_pairs
     quarter = keep_x.shape[2]
-    halves = [slice(0, n_pairs // 2), slice(n_pairs // 2, n_pairs)]
+    n_part = rd_s.shape[0]
+    n_each = n_pairs // n_part
+    halves = [slice(h * n_each, (h + 1) * n_each) for h in range(n_part)]
+    n_grp = st_scr.shape[0]
+    per_grp = n_pairs // n_grp
     me = lax.axis_index("cp")
     core = lax.rem(me, 2)
     chip = lax.div(me, 2)
@@ -115,9 +119,15 @@
     def chip_copies(k):
         out, at = [], 0
         for n, ref in enumerate((chip0_ref, chip1_ref, chip2_ref, chip3_ref)):
-            out.append(pltpu.make_async_copy(e_scr.at[k, at:at + ref.shape[0], :], ref.at[:, cols(k)], chip_sem.at[n, k]))
+            out.append(pltpu.make_async_copy(e_scr.at[k, at:at + ref.shape[0], :], ref.at[:, cols(k - 1)], chip_sem.at[n, k]))
             at += ref.shape[0]
         return out
+
+    def head_copy():
+        return pltpu.make_async_copy(e_scr.at[0], head_ref, head_sem.at[0])
+
+    def head_across():
+        return send(e_scr.at[0], head_got, (xd_s, xd_r), 0, across)
 
     def out_copies():
         return [pltpu.make_async_copy(full_oq.at[k, p], oq_ref.at[p, :, k * PAIR:(k + 1) * PAIR], out_sem.at[p, k])
@@ -127,8 +137,10 @@
         slot = lax.rem(g, 2)
         return pltpu.make_async_copy(pg_scr.at[slot], pg_ref.at[pl.ds(g * n_blk, n_blk)], pg_sem.at[slot])
 
-    def stats_copy(k):
-        return send(st_scr, other.at[k], (st_s, st_r), k, peers[k])
+    def stats_copies(q):
+        return [pltpu.make_async_remote_copy(
+            src_ref=st_scr.at[q], dst_ref=other.at[k, q], send_sem=st_s.at[k, q], recv_sem=st_r.at[k, q],
+            device_id={"cp": peers[k]}, device_id_type=pl.DeviceIdType.MESH) for k in range(n_cp - 1)]
 
     def oq_mate(h):
         return send(theirs_oq.at[halves[h]], got_oq.at[halves[h]], (rd_s, rd_r), h, mate)
@@ -167,8 +179,7 @@
     for c in act_copies():
         c.start()
 
-    @pl.loop(0, n_pairs)
-    def _(k):
+    for k in range(2):
         for c in weight_copies(k):
             c.start()
 
@@ -183,9 +194,11 @@
 
     @pl.loop(0, n_pairs)
     def _(i):
-        @pl.when((i > 0) & (i < n_pairs - 1))
-        def _():
-            mem_copy(i - 1).start()
+        @pl.when(i < n_pairs - 2)
+        def _():
+            for c in weight_copies(i + 2):
+                c.start()
+            mem_copy(i).start()
 
         for c in weight_copies(i):
             c.wait()
@@ -204,12 +217,21 @@
     for c in q_copies():
         c.start()
 
+    pl.semaphore_wait(barrier, n_cp - 1)
+
     @pl.loop(0, n_pairs)
     def _(g):
+        grp = lax.div(g, per_grp)
+
+        @pl.when((g > 0) & (lax.rem(g, per_grp) == 0))
+        def _():
+            for c in stats_copies(grp - 1):
+                c.start()
+
         mem_copy(g).wait()
         for j in range(n_blk):
             b = g * n_blk + j
-            at = pl.ds(b, 1)
+            at = pl.ds(lax.rem(g, per_grp) * n_blk + j, 1)
             t = dot(m_scr[b], zg_scr[:, :, seq_rows(b), :].reshape(2 * rows, width), NT)
             s = t[:, :rows] * scale
             dp = t[:, rows:] + ps_scr[:, seq_rows(b), :].reshape(rows, PAIR).T[0:1, :]
@@ -217,18 +239,22 @@
             e = jnp.exp(s - mx)
             e_scr[g, j * n_fr:(j + 1) * n_fr, :] = e
             dp_scr[g, j * n_fr:(j + 1) * n_fr, :] = dp
-            st_scr[0, at, :] = mx
-            st_scr[1, at, :] = jnp.sum(e, axis=0, keepdims=True)
-            st_scr[2, at, :] = jnp.sum(e * dp, axis=0, keepdims=True)
-
-    pl.semaphore_wait(barrier, n_cp - 1)
-    for k in range(n_cp - 1):
-        stats_copy(k).start()
-    for k in range(n_cp - 1):
-        stats_copy(k).wait()
+            st_scr[grp, 0, at, :] = mx
+            st_scr[grp, 1, at, :] = jnp.sum(e, axis=0, keepdims=True)
+            st_scr[grp, 2, at, :] = jnp.sum(e * dp, axis=0, keepdims=True)
+
+    for c in stats_copies(n_grp - 1):
+        c.start()
 
     @pl.loop(0, n_pairs)
     def _(g):
+        grp = lax.div(g, per_grp)
+
+        @pl.when(lax.rem(g, per_grp) == 0)
+        def _():
+            for c in stats_copies(grp):
+                c.wait()
+
         @pl.when(g >= 2)
         def _():
             pg_copy(g - 2).wait()
@@ -237,10 +263,8 @@
         ones = jnp.ones((n_fr, PAIR), BF16)
         for j in range(n_blk):
             b = g * n_blk + j
-            at = pl.ds(b, 1)
-            tops = [st_scr[0, at, :]] + [other[k, 0, at, :] for k in range(n_cp - 1)]
-            sums_l = [st_scr[1, at, :]] + [other[k, 1, at, :] for k in range(n_cp - 1)]
-            sums_c = [st_scr[2, at, :]] + [other[k, 2, at, :] for k in range(n_cp - 1)]
+            at = pl.ds(lax.rem(g, per_grp) * n_blk + j, 1)
+            tops, sums_l, sums_c = ([st_scr[grp, n, at, :]] + [other[k, grp, n, at, :] for k in range(n_cp - 1)] for n in range(3))
             top = functools.reduce(jnp.maximum, tops)
             fac = [jnp.exp(t - top) for t in tops]
             total = functools.reduce(jnp.add, [f * v for f, v in zip(fac, sums_l)])
@@ -265,19 +289,15 @@
             mine_oq[k, part] = jnp.where(first, top, bottom)
             theirs_oq[k, part] = jnp.where(first, bottom, top)
 
-    @pl.loop(0, n_pairs // 2)
-    def _(k):
-        o_and_dq(k)
-
-    oq_mate(0).start()
-
-    @pl.loop(n_pairs // 2, n_pairs)
-    def _(k):
-        o_and_dq(k)
-
-    oq_mate(1).start()
-    add_mate(0)
-    oq_across(0).start()
+    for h in range(n_part):
+        @pl.loop(h * n_each, (h + 1) * n_each)
+        def _(k):
+            o_and_dq(k)
+
+        oq_mate(h).start()
+        if h > 0:
+            add_mate(h - 1)
+            oq_across(h - 1).start()
 
     def close_dw(k):
         dw_mate(k).wait()
@@ -289,11 +309,15 @@
         def _():
             dw_mate(k - 1).start()
 
-        @pl.when(k == 3)
-        def _():
-            oq_across(1).start()
-
-        @pl.when(k >= 5)
+        @pl.when(k == 2)
+        def _():
+            oq_across(n_part - 1).start()
+
+        @pl.when(k == 5)
+        def _():
+            head_copy().start()
+
+        @pl.when(k >= 6)
         def _():
             for c in chip_copies(k - 5):
                 c.start()
@@ -304,9 +328,9 @@
         e_scr[k] = jnp.where(first, dwk, dwv)
         dp_scr[k] = jnp.where(first, dwv, dwk)
 
-        @pl.when(k == 2)
-        def _():
-            add_mate(1)
+        @pl.when(k == 1)
+        def _():
+            add_mate(n_part - 1)
 
         @pl.when(k >= 4)
         def _():
@@ -323,54 +347,60 @@
         for c in chip_copies(k):
             c.start()
 
-    finish(0)
-    own_across(0).start()
-    finish(1)
-    own_across(1).start()
+    for h in range(n_part):
+        finish(h)
+        own_across(h).start()
     for k in range(n_cp - 1):
         small_copy(k).start()
-    own_across(0).wait()
-    half_mate(0).start()
-    own_across(1).wait()
-    half_mate(1).start()
+    head_across().start()
+    for h in range(n_part):
+        own_across(h).wait()
+        half_mate(h).start()
     for k in range(n_cp - 1):
         small_copy(k).wait()
     small_ref[...] = small_scr[0] + small_scr[1] + small_scr[2] + small_scr[3]
-    half_mate(0).wait()
-    half_mate(1).wait()
+    for h in range(n_part):
+        half_mate(h).wait()
     for c in out_copies():
         c.start()
 
-    @pl.loop(0, n_pairs)
+    @pl.loop(1, n_pairs)
     def _(k):
         for c in chip_copies(k):
             c.wait()
 
+    head_copy().wait()
     for g in (n_pairs - 2, n_pairs - 1):
         pg_copy(g).wait()
     for c in q_copies() + out_copies():
         c.wait()
-
-
-def assemble_kernel(core_ref, fin_ref, other_ref, *refs):
+    head_across().wait()
+
+
+def assemble_kernel(core_ref, own_ref, got_ref, own2_ref, got2_ref, head_ref, head2_ref, *refs):
     wk_ref, wv_ref = refs[-2:]
     first = core_ref[0] == 0
-    wk_ref[...] = jnp.where(first, fin_ref[...], other_ref[...])
-    wv_ref[...] = jnp.where(first, other_ref[...], fin_ref[...])
-
-
-def assemble(core, fin, other, at, acc):
-    n, width = fin.shape
-    step = 192 if n % 192 == 0 and at % 192 == 0 else 64
-    block = pl.BlockSpec((step, width), lambda i: (i, 0))
+    mine, other = own_ref[...] + got_ref[...], own2_ref[...] + got2_ref[...]
+    wk_ref[:, :PAIR] = jnp.where(first, head_ref[...], head2_ref[...])
+    wv_ref[:, :PAIR] = jnp.where(first, head2_ref[...], head_ref[...])
+    wk_ref[:, PAIR:] = jnp.where(first, mine, other)
+    wv_ref[:, PAIR:] = jnp.where(first, other, mine)
+
+
+def assemble(core, own, got, own2, got2, head, head2, at, acc):
+    n, width = own.shape[0], own.shape[1] + PAIR
+    step = next(k for k in (192, 128, 64) if n % k == 0 and at % k == 0)
+    block = pl.BlockSpec((step, width - PAIR), lambda i: (i, 0))
+    head_block = pl.BlockSpec((step, PAIR), lambda i: (at // step + i, 0))
     out = pl.BlockSpec((step, width), lambda i: (at // step + i, 0))
     return pl.pallas_call(
         assemble_kernel, grid=(n // step,), name="assemble",
-        in_specs=[pl.BlockSpec(memory_space=pltpu.SMEM), block, block] + [pl.BlockSpec(memory_space=pl.ANY)] * len(acc),
+        in_specs=[pl.BlockSpec(memory_space=pltpu.SMEM)] + [block] * 4 + [head_block] * 2
+        + [pl.BlockSpec(memory_space=pl.ANY)] * len(acc),
         out_specs=[out, out], out_shape=[jax.ShapeDtypeStruct((width, width), F32)] * 2,
-        input_output_aliases={3: 0, 4: 1} if acc else {},
-        compiler_params=pltpu.CompilerParams(dimension_semantics=("arbitrary",)),
-    )(core, fin, other, *acc)
+        input_output_aliases={7: 0, 8: 1} if acc else {},
+        compiler_params=params(),
+    )(core, own, got, own2, got2, head, head2, *acc)
 
 
 def mem_kernel(n_first, q2_ref, d2_ref, wk_ref, wv_ref, pg_ref, dm_ref, z_scr):
@@ -421,7 +451,7 @@
         h2, gy2 = hidden.reshape(tokens, width), grad_y.reshape(tokens, width)
         blk = n_seq // n_pairs
         quarter = tokens // 4
-        chunks = [width * 3 // 8, width * 3 // 8, width * 3 // 16, width // 16]
+        chunks = [width * 3 // 8, width * 5 // 16, width * 3 // 16, width // 8]
         anywhere = pl.BlockSpec(memory_space=pl.ANY)
         vm = lambda dt, *s: pltpu.VMEM(s, dt)
         sems = lambda *n: pltpu.SemaphoreType.DMA(n)
@@ -429,9 +459,10 @@
         pg, *rest = pl.pallas_call(
             functools.partial(fused_kernel, scale, n_cp), name="fused",
             in_specs=[anywhere] * 7 + [pl.BlockSpec(memory_space=pltpu.VMEM)] * 4,
-            out_specs=[anywhere] * 8 + [pl.BlockSpec(memory_space=pltpu.VMEM)],
+            out_specs=[anywhere] * 10 + [pl.BlockSpec(memory_space=pltpu.VMEM)],
             out_shape=[jax.ShapeDtypeStruct((n_seq, n_fr, 2 * rows), BF16)]
-            + [jax.ShapeDtypeStruct((c, width), F32) for c in chunks]
+            + [jax.ShapeDtypeStruct((c, width - PAIR), F32) for c in chunks]
+            + [jax.ShapeDtypeStruct((width, PAIR), F32)] * 2
             + [jax.ShapeDtypeStruct((2, tokens, width), BF16)]
             + [jax.ShapeDtypeStruct((n_pairs, 2 * tokens, PAIR), BF16)] * 2
             + [jax.ShapeDtypeStruct((2, n_pairs, PAIR), F32)],
@@ -440,25 +471,29 @@
                             vm(F32, n_pairs, blk * n_fr, rows), vm(F32, n_pairs, blk * n_fr, rows),
                             vm(BF16, width, width), vm(BF16, width, width), vm(F32, n_pairs, 2 * tokens, PAIR),
                             vm(BF16, n_pairs, 2 * tokens, PAIR), vm(BF16, n_pairs, 2 * tokens, PAIR),
-                            vm(F32, 3, n_seq, rows), vm(F32, n_cp - 1, 3, n_seq, rows),
+                            vm(F32, 4, 3, n_seq // 4, rows), vm(F32, n_cp - 1, 4, 3, n_seq // 4, rows),
                             vm(F32, n_pairs, 2, 2 * quarter, PAIR), vm(F32, n_pairs, 2, 2 * quarter, PAIR),
                             vm(F32, n_pairs, 2, 2 * quarter, PAIR), vm(F32, n_pairs, 2, quarter, PAIR),
                             vm(F32, n_pairs, 2, quarter, PAIR), vm(F32, n_pairs, 2, quarter, PAIR),
                             vm(BF16, n_pairs, 2, tokens, PAIR), vm(F32, n_cp, 2, n_pairs, PAIR),
                             vm(F32, n_pairs, width, PAIR),
-                            sems(2), sems(4, n_pairs), sems(n_pairs), sems(2), sems(4, n_pairs), sems(2, n_pairs),
+                            sems(2), sems(4, n_pairs), sems(n_pairs), sems(2), sems(4, n_pairs), sems(1), sems(2, n_pairs),
                             sems(2), vm(BF16, 2, blk, n_fr, 2 * rows)]
-            + both(n_cp - 1) + both(2) + both(2) + both(2) + both(2) + both(n_pairs) + both(n_cp - 1),
+            + [sems(n_cp - 1, 4)] * 2 + both(4) + both(4) + both(4) + both(4) + both(n_pairs) + both(n_cp - 1) + both(1),
             compiler_params=pltpu.CompilerParams(vmem_limit_bytes=VMEM_LIMIT, collective_id=0, has_side_effects=True),
         )(h2, gy2, w_q.reshape(blk, n_fr, width), w_k, w_v, w_o.reshape(blk, n_fr, width), memory, ln_gain, ln_bias, b_q, b_v)
-        chips, (oq, q2, d2, small) = rest[:4], rest[4:]
+        chips, (head, head_got, oq, q2, d2, small) = rest[:4], rest[4:]
         attn_out, dq_low = oq[0], oq[1]
         small = small.reshape(2, width)
         grad_bq, grad_bv = small[0], small[1]
 
-        got = []
+        got, chips2 = [], []
         for c in chips:
             got.append(swap(c, 2))
+        for c in chips:
+            chips2.append(swap(c, 1))
+        head = head + head_got
+        head2 = swap(head, 1)
 
         hidden_f32 = h2.astype(F32)
         centered = hidden_f32 - jnp.mean(hidden_f32, axis=-1, keepdims=True)
@@ -493,10 +528,9 @@
         out_y, grad_h, grad_mem, grad_ln_gain, grad_ln_bias, grad_wq, grad_wo, grad_bo = hidden_work
         core_arr = core.reshape(1).astype(jnp.int32)
         acc, at = (), 0
-        for c, g in zip(chips, got):
+        for c, c2, g in zip(chips, chips2, got):
             g, acc = lax.optimization_barrier((g, acc))
-            fin = c + g
-            acc = assemble(core_arr, fin, swap(fin, 1), at, acc)
+            acc = assemble(core_arr, c, g, c2, swap(g, 1), head, head2, at, acc)
             at += c.shape[0]
         grad_wk, grad_wv = acc
         return (out_y.reshape(hidden.shape), grad_h.reshape(hidden.shape), grad_mem, grad_ln_gain, grad_ln_bias,

time: 173 us -> 164 us (0.948)
  waiting for transfers between devices: 50.9 us -> 37.6 us
  Pallas kernels: 87.8 us -> 98.4 us
  other arithmetic: 11.3 us -> 6.4 us
    ppermute x8 -> x13, waiting for transfers between devices: 50.9 us -> 37.6 us  [swap(): return lax.ppermute(x, 'cp', [(i, i ^ bit) for i in range(n_cp)])]
    pallas_call x1, Pallas kernels: 58.3 us -> 64 us  [device_step(): pl.pallas_call(functools.partial(fused_kernel, scale, n_cp), name='fused'...]
    pallas_call x4, Pallas kernels: 10.8 us -> 15.7 us  [assemble(): pl.pallas_call(assemble_kernel, grid=(n // step,), name='assemble', in_sp...]
    add x4 -> x1, other arithmetic: 5.42 us -> 1.25 us  [device_step(): head = head + head_got]
    ppermute x8 -> x13, starting transfers between devices: 7.15 us -> 7 us  [swap(): return lax.ppermute(x, 'cp', [(i, i ^ bit) for i in range(n_cp)])]
  transfers between devices with their start and end apart: 8 -> 13, of which waited for: 7 -> 7; matrix products, arithmetic and copies ran while one was open for 10% -> 11% of each run, Pallas kernels for 16% -> 19%
where the time goes in v1:
time: 164 us; the launch traced here: 163 us
  Pallas kernels  98.4 us (60%)
  waiting for transfers between devices  37.6 us (23%)
  matrix products  10.1 us (6%)
  starting transfers between devices  7 us (4%)
  other arithmetic  6.4 us (4%)
  local copies, waits for them, and re-layouts  3.11 us (2%)
    pallas_call x1, Pallas kernels, device_step(): pl.pallas_call(functools.partial(fused_kernel, scale, n_cp), name='fused'...  64 us
    ppermute x13, waiting for transfers between devices, swap(): return lax.ppermute(x, 'cp', [(i, i ^ bit) for i in range(n_cp)])  37.6 us
    pallas_call x1, Pallas kernels, device_step(): pl.pallas_call(functools.partial(mem_kernel, n_pairs), grid=(2 * n_pairs,...  18.6 us
    pallas_call x4, Pallas kernels, assemble(): pl.pallas_call(assemble_kernel, grid=(n // step,), name='assemble', in_sp...  15.7 us
    dot_general x4, matrix products, dot(): return lax.dot_general(a, b, dims, preferred_element_type=F32)  10.1 us
    ppermute x13, starting transfers between devices, swap(): return lax.ppermute(x, 'cp', [(i, i ^ bit) for i in range(n_cp)])  7 us
  transfers between devices with their start and end apart: 13, of which 7 were waited for; matrix products, arithmetic and copies ran while one was open for 11% of the time, Pallas kernels for 19%

profile of v1, /device:TPU:0, one launch (start us, length us, event | category | flops | bytes accessed | tf_op | source)
XLA Modules:
  0.0 163.3 jit_solution(15793311353748718830)
XLA Ops:
  0.6 64.0 %fused.1 = (bf16[32,256,256]{2,1,0:T(8,128)(2,1)}, f32[384,896]{1,0:T(8,128)}, f32[320,896]{1,0:T(8,128)}, f32[192,896]{1,0:T(8,128)}, f32[128,896]{1,0:T(8,128)...) custom-call(bf16[256,1024]{1,0:T(8,128)(2,1)} %bitcast.35, ...), custom_call_target="tpu_custom_call" | custom-call | tf_op jit(solution)/shard_map/fused/pallas_call | solution.py:459
  64.7 0.0 collective-permute-start
  64.7 0.0 collective-permute-start.4
  64.8 1.2 convert_reduce_fusion
  66.0 1.3 fusion.4
  67.3 0.1 div.17
  67.4 0.7 convert_element_type.41
  68.1 0.1 rsqrt.13
  68.2 0.0 copy-start.8
  68.2 0.0 copy-start
  68.2 0.0 copy-start.4
  68.2 0.0 copy-start.6
  68.2 4.1 %fusion.24 = f32[1024,1024]{1,0:T(8,128)} fusion(bf16[2,256,1024]{2,1,0:T(8,128)(2,1)} %get-tuple-element.50, bf16[32,8,1024]{2,1,0:T(8,128)(2,1)} %param.23), kind=kOutput, calls=%fused_computation.29 | convolution fusion | flops 536870912 | bytes 5242880 | tf_op jit(solution)/shard_map/dot_general | solution.py:23
  72.3 0.0 copy-done.8
  72.3 0.0 copy-done
  72.3 0.0 copy-done.4
  72.3 0.0 copy-done.6
  72.3 0.0 copy-start.5
  72.4 1.5 fusion.1
  73.9 0.0 copy-done.5
  73.9 0.0 copy-start.2
  73.9 1.6 fusion.17
  75.5 0.0 copy-start.7
  75.5 0.0 copy-done.2
  75.5 1.2 fusion.16
  76.8 0.0 copy-done.7
  76.8 0.7 convert_reduce_fusion.1
  77.5 2.9 %fusion.19 = f32[1024,1024]{1,0:T(8,128)} fusion(bf16[32,8,1024]{2,1,0:T(8,128)(2,1)S(1)} %copy-done, f32[1024]{0:T(1024)S(1)} %convert_element_type.43, f32[1024]{0:T(1024)S(1)} %convert_element_type.41, f32[32,8]{1,0:T(8,128)S(1)} %add_rsqrt_fusion, f32[32,8]{1,0:T(8,128)S(1)} %broadcast_multiply_fusion, bf16[2,256,1024]{2,1,0:T(8,128)(2,1)S(1)} %copy-done.6), kind=kOutput, calls=%fused_computation.25 | convolution fusion | flops 538443776 | bytes 5283840 | tf_op jit(solution)/shard_map/dot_general | solution.py:23
  80.4 18.6 %mem.1 = bf16[32,256,1024]{2,1,0:T(8,128)(2,1)} custom-call(bf16[8,512,128]{2,1,0:T(8,128)(2,1)} %get-tuple-element.51.q2_ref, bf16[8,512,128]{2,1,0:T(8,128)(2,1)} %get-tuple-element.52.d2_ref, bf16[1024,1024]{1,0:T(8,128)(2,1)} %wk_ref.3, bf16[1024,1024]{1,0:T(8,128)(2,1)} %wv_ref.3, bf16[32,256,256]{2,1,0:T(8,128)(2,1)} %get-tuple-element.53.pg_ref), custom_call_target="tpu_custom_call" | custom-call | flops 8589934592 | bytes 41943040 | tf_op jit(solution)/shard_map/mem/pallas_call | solution.py:518
  99.0 0.0 collective-permute-done.got_ref
  99.0 0.5 collective-permute-start.5
  99.5 2.0 %collective-permute-start.3 = (f32[320,896]{1,0:T(8,128)}, f32[320,896]{1,0:T(8,128)}, u32[]{:S(2)}, u32[]{:S(2)}) collective-permute-start(f32[320,896]{1,0:T(8,128)} %get-tuple-element.63.own_ref), channel_id=1, source_target_pairs={{0,2},{1,3},{2,0},{3,1},{4,6},{5,7},{6,4},{7,5},{8,10},{9,11},{10,... | collective-permute-start | bytes 3440648 | tf_op jit(solution)/shard_map/ppermute | solution.py:440
  101.5 1.3 add.52.head_ref
  102.7 0.0 copy-start.1
  102.7 0.8 copy-done.1
  103.5 0.0 collective-permute-start.6
  103.5 0.5 collective-permute-start.7
  104.0 1.4 collective-permute-done.6.head2_ref
  105.4 0.0 copy-start.3
  105.4 0.8 copy-done.3
  106.2 0.0 collective-permute-done.4.own2_ref
  106.2 0.0 collective-permute-done.5.got2_ref
  106.2 4.0 %assemble.4 = (f32[1024,1024]{1,0:T(8,128)}, f32[1024,1024]{1,0:T(8,128)}) custom-call(s32[1]{0:T(128)} %bitcast.10.core_ref, f32[384,896]{1,0:T(8,128)} %get-tuple-element.49.own_ref, f32[384,896]{1,0:T(8,128)} %collective-permute-done.got_ref, f32[384,896]{1,0:T(8,128)} %collective-permute-done.4.own2_ref, f32[384,896]{1,0:T(8,128)} %collective-permute-done.5.got2_ref, ...), custom_call_target="tpu_custom_call" | custom-call | tf_op jit(solution)/shard_map/assemble/pallas_call | solution.py:396
  110.2 17.0 %collective-permute-done.3.got_ref = f32[320,896]{1,0:T(8,128)} collective-permute-done((f32[320,896]{1,0:T(8,128)}, f32[320,896]{1,0:T(8,128)}, u32[]{:S(2)}, u32[]{:S(2)}) %collective-permute-start.3) | collective-permute-done | bytes 1146912 | tf_op jit(solution)/shard_map/ppermute | solution.py:440
  127.3 0.0 collective-permute-start.8
  127.3 1.7 %collective-permute-start.2 = (f32[192,896]{1,0:T(8,128)}, f32[192,896]{1,0:T(8,128)}, u32[]{:S(2)}, u32[]{:S(2)}) collective-permute-start(f32[192,896]{1,0:T(8,128)} %get-tuple-element.62.own_ref), channel_id=1, source_target_pairs={{0,2},{1,3},{2,0},{3,1},{4,6},{5,7},{6,4},{7,5},{8,10},{9,11},{10,... | collective-permute-start | bytes 2064392 | tf_op jit(solution)/shard_map/ppermute | solution.py:440
  129.0 0.2 collective-permute-start.9
  129.2 0.0 collective-permute-done.7.own2_ref
  129.2 1.2 collective-permute-done.8.got2_ref
  130.4 5.4 %assemble.5 = (f32[1024,1024]{1,0:T(8,128)}, f32[1024,1024]{1,0:T(8,128)}) custom-call(s32[1]{0:T(128)} %bitcast.10.core_ref, f32[320,896]{1,0:T(8,128)} %get-tuple-element.63.own_ref, f32[320,896]{1,0:T(8,128)} %collective-permute-done.3.got_ref, f32[320,896]{1,0:T(8,128)} %collective-permute-done.7.own2_ref, ...), custom_call_target="tpu_custom_call", output_to_operand_aliasing={{0}: (7, {}), {1}: (8, {})} | custom-call | tf_op jit(solution)/shard_map/assemble/pallas_call | solution.py:396
  135.8 9.6 %collective-permute-done.2.got_ref = f32[192,896]{1,0:T(8,128)} collective-permute-done((f32[192,896]{1,0:T(8,128)}, f32[192,896]{1,0:T(8,128)}, u32[]{:S(2)}, u32[]{:S(2)}) %collective-permute-start.2) | collective-permute-done | bytes 688160 | tf_op jit(solution)/shard_map/ppermute | solution.py:440
  145.4 0.0 collective-permute-start.10
  145.4 1.7 %collective-permute-start.1 = (f32[128,896]{1,0:T(8,128)}, f32[128,896]{1,0:T(8,128)}, u32[]{:S(2)}, u32[]{:S(2)}) collective-permute-start(f32[128,896]{1,0:T(8,128)} %get-tuple-element.61.own_ref), channel_id=1, source_target_pairs={{0,2},{1,3},{2,0},{3,1},{4,6},{5,7},{6,4},{7,5},{8,10},{9,11},{10,... | collective-permute-start | bytes 1376264 | tf_op jit(solution)/shard_map/ppermute | solution.py:440
  147.2 0.2 collective-permute-start.11
  147.4 0.0 collective-permute-done.9.own2_ref
  147.4 0.5 collective-permute-done.10.got2_ref
  147.9 3.8 %assemble.6 = (f32[1024,1024]{1,0:T(8,128)}, f32[1024,1024]{1,0:T(8,128)}) custom-call(s32[1]{0:T(128)} %bitcast.10.core_ref, f32[192,896]{1,0:T(8,128)} %get-tuple-element.62.own_ref, f32[192,896]{1,0:T(8,128)} %collective-permute-done.2.got_ref, f32[192,896]{1,0:T(8,128)} %collective-permute-done.9.own2_ref, ...), custom_call_target="tpu_custom_call", output_to_operand_aliasing={{0}: (7, {}), {1}: (8, {})} | custom-call | tf_op jit(solution)/shard_map/assemble/pallas_call | solution.py:396
  151.7 7.0 %collective-permute-done.1.got_ref = f32[128,896]{1,0:T(8,128)} collective-permute-done((f32[128,896]{1,0:T(8,128)}, f32[128,896]{1,0:T(8,128)}, u32[]{:S(2)}, u32[]{:S(2)}) %collective-permute-start.1) | collective-permute-done | bytes 458784 | tf_op jit(solution)/shard_map/ppermute | solution.py:440
  158.7 0.0 collective-permute-start.12
  158.7 1.3 slice_bitcast_fusion
  160.0 0.0 collective-permute-done.11.own2_ref
  160.0 0.9 collective-permute-done.12.got2_ref
  160.8 2.5 %assemble.7 = (f32[1024,1024]{1,0:T(8,128)}, f32[1024,1024]{1,0:T(8,128)}) custom-call(s32[1]{0:T(128)} %bitcast.10.core_ref, f32[128,896]{1,0:T(8,128)} %get-tuple-element.61.own_ref, f32[128,896]{1,0:T(8,128)} %collective-permute-done.1.got_ref, f32[128,896]{1,0:T(8,128)} %collective-permute-done.11.own2_ref, ...), custom_call_target="tpu_custom_call", output_to_operand_aliasing={{0}: (7, {}), {1}: (8, {})} | custom-call | tf_op jit(solution)/shard_map/assemble/pallas_call | solution.py:396
  (5 shorter events, 0.0 us)
Async XLA Ops:
  64.7 34.3 %collective-permute-start = (f32[384,896]{1,0:T(8,128)}, f32[384,896]{1,0:T(8,128)}, u32[]{:S(2)}, u32[]{:S(2)}) collective-permute-start(f32[384,896]{1,0:T(8,128)} %get-tuple-element.49.own_ref), channel_id=1, source_target_pairs={{0,2},{1,3},{2,0},{3,1},{4,6},{5,7},{6,4},{7,5},{8,10},{9,11},{10,... | collective-permute-start | bytes 4128776 | tf_op jit(solution)/shard_map/ppermute | solution.py:440
  64.7 41.5 %collective-permute-start.4 = (f32[384,896]{1,0:T(8,128)}, f32[384,896]{1,0:T(8,128)}, u32[]{:S(2)}, u32[]{:S(2)}) collective-permute-start(f32[384,896]{1,0:T(8,128)} %get-tuple-element.49.own_ref), channel_id=1, source_target_pairs={{0,1},{1,0},{2,3},{3,2},{4,5},{5,4},{6,7},{7,6},{8,9},{9,8},{10,11... | collective-permute-start | bytes 4128776 | tf_op jit(solution)/shard_map/ppermute | solution.py:440
  68.2 4.2 %copy-start.8 = (bf16[1024]{0:T(1024)(128)(2,1)S(1)}, bf16[1024]{0:T(1024)(128)(2,1)}, u32[]{:S(2)}) copy-start(bf16[1024]{0:T(1024)(128)(2,1)} %param.22) | copy-start | bytes 6148
  68.2 4.2 %copy-start = (bf16[32,8,1024]{2,1,0:T(8,128)(2,1)S(1)}, bf16[32,8,1024]{2,1,0:T(8,128)(2,1)}, u32[]{:S(2)}) copy-start(bf16[32,8,1024]{2,1,0:T(8,128)(2,1)} %param.12) | copy-start | bytes 1572868
  68.2 4.1 %copy-start.4 = (bf16[1024,1024]{1,0:T(8,128)(2,1)S(1)}, bf16[1024,1024]{1,0:T(8,128)(2,1)}, u32[]{:S(2)}) copy-start(bf16[1024,1024]{1,0:T(8,128)(2,1)} %param.21) | copy-start | bytes 6291460
  68.2 4.1 %copy-start.6 = (bf16[2,256,1024]{2,1,0:T(8,128)(2,1)S(1)}, bf16[2,256,1024]{2,1,0:T(8,128)(2,1)}, u32[]{:S(2)}) copy-start(bf16[2,256,1024]{2,1,0:T(8,128)(2,1)} %get-tuple-element.50) | copy-start | bytes 3145732
  72.3 1.6 copy-start.5
  73.9 1.6 copy-start.2
  75.5 1.3 copy-start.7
  99.0 7.2 %collective-permute-start.5 = (f32[384,896]{1,0:T(8,128)}, f32[384,896]{1,0:T(8,128)}, u32[]{:S(2)}, u32[]{:S(2)}) collective-permute-start(f32[384,896]{1,0:T(8,128)} %collective-permute-done.got_ref), channel_id=1, source_target_pairs={{0,1},{1,0},{2,3},{3,2},{4,5},{5,4},{6,7},{7,6},{8,9},{9,8},{10,11... | collective-permute-start | bytes 4128776 | tf_op jit(solution)/shard_map/ppermute | solution.py:440
  99.5 27.8 %collective-permute-start.3 = (f32[320,896]{1,0:T(8,128)}, f32[320,896]{1,0:T(8,128)}, u32[]{:S(2)}, u32[]{:S(2)}) collective-permute-start(f32[320,896]{1,0:T(8,128)} %get-tuple-element.63.own_ref), channel_id=1, source_target_pairs={{0,2},{1,3},{2,0},{3,1},{4,6},{5,7},{6,4},{7,5},{8,10},{9,11},{10,... | collective-permute-start | bytes 3440648 | tf_op jit(solution)/shard_map/ppermute | solution.py:440
  102.7 0.8 copy-start.1
  103.5 1.9 %collective-permute-start.6 = (f32[1024,128]{1,0:T(8,128)S(1)}, f32[1024,128]{1,0:T(8,128)S(1)}, u32[]{:S(2)}, u32[]{:S(2)}) collective-permute-start(f32[1024,128]{1,0:T(8,128)S(1)} %add.52.head_ref), channel_id=1, source_target_pairs={{0,1},{1,0},{2,3},{3,2},{4,5},{5,4},{6,7},{7,6},{8,9},{9,8},{10,11... | collective-permute-start | bytes 1572872 | tf_op jit(solution)/shard_map/ppermute | solution.py:440
  103.5 25.7 %collective-permute-start.7 = (f32[320,896]{1,0:T(8,128)}, f32[320,896]{1,0:T(8,128)}, u32[]{:S(2)}, u32[]{:S(2)}) collective-permute-start(f32[320,896]{1,0:T(8,128)} %get-tuple-element.63.own_ref), channel_id=1, source_target_pairs={{0,1},{1,0},{2,3},{3,2},{4,5},{5,4},{6,7},{7,6},{8,9},{9,8},{10,11... | collective-permute-start | bytes 3440648 | tf_op jit(solution)/shard_map/ppermute | solution.py:440
  105.4 0.8 copy-start.3
  127.3 3.1 %collective-permute-start.8 = (f32[320,896]{1,0:T(8,128)}, f32[320,896]{1,0:T(8,128)}, u32[]{:S(2)}, u32[]{:S(2)}) collective-permute-start(f32[320,896]{1,0:T(8,128)} %collective-permute-done.3.got_ref), channel_id=1, source_target_pairs={{0,1},{1,0},{2,3},{3,2},{4,5},{5,4},{6,7},{7,6},{8,9},{9,8},{10,11... | collective-permute-start | bytes 3440648 | tf_op jit(solution)/shard_map/ppermute | solution.py:440
  127.3 18.2 %collective-permute-start.2 = (f32[192,896]{1,0:T(8,128)}, f32[192,896]{1,0:T(8,128)}, u32[]{:S(2)}, u32[]{:S(2)}) collective-permute-start(f32[192,896]{1,0:T(8,128)} %get-tuple-element.62.own_ref), channel_id=1, source_target_pairs={{0,2},{1,3},{2,0},{3,1},{4,6},{5,7},{6,4},{7,5},{8,10},{9,11},{10,... | collective-permute-start | bytes 2064392 | tf_op jit(solution)/shard_map/ppermute | solution.py:440
  129.0 18.4 %collective-permute-start.9 = (f32[192,896]{1,0:T(8,128)}, f32[192,896]{1,0:T(8,128)}, u32[]{:S(2)}, u32[]{:S(2)}) collective-permute-start(f32[192,896]{1,0:T(8,128)} %get-tuple-element.62.own_ref), channel_id=1, source_target_pairs={{0,1},{1,0},{2,3},{3,2},{4,5},{5,4},{6,7},{7,6},{8,9},{9,8},{10,11... | collective-permute-start | bytes 2064392 | tf_op jit(solution)/shard_map/ppermute | solution.py:440
  145.4 2.5 %collective-permute-start.10 = (f32[192,896]{1,0:T(8,128)}, f32[192,896]{1,0:T(8,128)}, u32[]{:S(2)}, u32[]{:S(2)}) collective-permute-start(f32[192,896]{1,0:T(8,128)} %collective-permute-done.2.got_ref), channel_id=1, source_target_pairs={{0,1},{1,0},{2,3},{3,2},{4,5},{5,4},{6,7},{7,6},{8,9},{9,8},{10,11... | collective-permute-start | bytes 2064392 | tf_op jit(solution)/shard_map/ppermute | solution.py:440
  145.4 13.2 %collective-permute-start.1 = (f32[128,896]{1,0:T(8,128)}, f32[128,896]{1,0:T(8,128)}, u32[]{:S(2)}, u32[]{:S(2)}) collective-permute-start(f32[128,896]{1,0:T(8,128)} %get-tuple-element.61.own_ref), channel_id=1, source_target_pairs={{0,2},{1,3},{2,0},{3,1},{4,6},{5,7},{6,4},{7,5},{8,10},{9,11},{10,... | collective-permute-start | bytes 1376264 | tf_op jit(solution)/shard_map/ppermute | solution.py:440
  147.2 12.8 %collective-permute-start.11 = (f32[128,896]{1,0:T(8,128)}, f32[128,896]{1,0:T(8,128)}, u32[]{:S(2)}, u32[]{:S(2)}) collective-permute-start(f32[128,896]{1,0:T(8,128)} %get-tuple-element.61.own_ref), channel_id=1, source_target_pairs={{0,1},{1,0},{2,3},{3,2},{4,5},{5,4},{6,7},{7,6},{8,9},{9,8},{10,11... | collective-permute-start | bytes 1376264 | tf_op jit(solution)/shard_map/ppermute | solution.py:440
  158.7 2.2 %collective-permute-start.12 = (f32[128,896]{1,0:T(8,128)}, f32[128,896]{1,0:T(8,128)}, u32[]{:S(2)}, u32[]{:S(2)}) collective-permute-start(f32[128,896]{1,0:T(8,128)} %collective-permute-done.1.got_ref), channel_id=1, source_target_pairs={{0,1},{1,0},{2,3},{3,2},{4,5},{5,4},{6,7},{7,6},{8,9},{9,8},{10,11... | collective-permute-start | bytes 1376264 | tf_op jit(solution)/shard_map/ppermute | solution.py:440

commit v2 on v1

--- a/solution.py
+++ b/solution.py
@@ -61,9 +61,13 @@
         device_id={"cp": peer}, device_id_type=pl.DeviceIdType.MESH)
 
 
-def fused_kernel(scale, n_cp, h_ref, gy_ref, wq_ref, wk_ref, wv_ref, wo_ref, m_ref, gain_ref, bias_ref, bq_ref, bv_ref,
+def fused_kernel(scale, n_cp, h_ref, gy_ref, wq_ref, wk_ref, wv_ref, wo_ref, m_ref, *refs):
+    fused_body(scale, n_cp, h_ref, gy_ref, wq_ref, wk_ref, wv_ref, wo_ref, m_ref, refs[:4], *refs[4:])
+
+
+def fused_body(scale, n_cp, h_ref, gy_ref, wq_ref, wk_ref, wv_ref, wo_ref, m_ref, vec_refs,
                  pg_ref, chip0_ref, chip1_ref, chip2_ref, chip3_ref, head_ref, head_got, oq_ref, q2_out, d2_out, small_ref,
-                 x_scr, gy_scr, vec_scr, zg_scr, m_scr, e_scr, dp_scr, wk_scr, wv_scr, ps_scr, q2_scr, d2_scr, st_scr, other,
+                 x_scr, gy_scr, raw0, raw1, raw2, raw3, vec_scr, zg_scr, m_scr, e_scr, dp_scr, wk_scr, wv_scr, ps_scr, q2_scr, d2_scr, st_scr, other,
                  mine_oq, theirs_oq, got_oq, keep_x, give_x, got_x, full_oq, small_scr, got_dw,
                  in_sem, w_sem, m_sem, q_sem, chip_sem, head_sem, out_sem, pg_sem, pg_scr,
                  st_s, st_r, rd_s, rd_r, rx_s, rx_r, ax_s, ax_r, ad_s, ad_r, dw_s, dw_r, sm_s, sm_r, xd_s, xd_r):
@@ -87,7 +91,6 @@
     left = chip == 0
     peers = [lax.rem(me + d, n_cp) for d in range(1, n_cp)]
     wq_at, wo_at = n_seq - 2 * n_blk, n_seq - n_blk
-    per_row = n_fr // PAIR
 
     def cols(k):
         return pl.ds(pl.multiple_of(k * PAIR, PAIR), PAIR)
@@ -95,14 +98,13 @@
     def seq_rows(b):
         return pl.ds(pl.multiple_of(b * n_row, n_row), n_row)
 
-    def wo_rows(k):
-        return lax.div(k, per_row), pl.ds(pl.multiple_of(lax.rem(k, per_row) * PAIR, PAIR), PAIR)
+    def wide(k):
+        return pl.ds(pl.multiple_of(k * 2 * PAIR, 2 * PAIR), 2 * PAIR)
 
     def weight_copies(k):
-        c = cols(k)
-        block, r = wo_rows(k)
+        c = wide(k)
         return [pltpu.make_async_copy(wq_ref.at[:, :, c], m_scr.at[wq_at:wo_at, :, c], w_sem.at[0, k]),
-                pltpu.make_async_copy(wo_ref.at[block, r, :], m_scr.at[wo_at + block, r, :], w_sem.at[1, k]),
+                pltpu.make_async_copy(wo_ref.at[k], m_scr.at[wo_at + k], w_sem.at[1, k]),
                 pltpu.make_async_copy(wk_ref.at[:, c], wk_scr.at[:, c], w_sem.at[2, k]),
                 pltpu.make_async_copy(wv_ref.at[:, c], wv_scr.at[:, c], w_sem.at[3, k])]
 
@@ -111,7 +113,8 @@
         return pltpu.make_async_copy(m_ref.at[at], m_scr.at[at], m_sem.at[g])
 
     def act_copies():
-        return [pltpu.make_async_copy(h_ref, x_scr, in_sem.at[0]), pltpu.make_async_copy(gy_ref, gy_scr, in_sem.at[1])]
+        return [pltpu.make_async_copy(src, dst, in_sem.at[k]) for k, (src, dst) in enumerate(
+            zip((h_ref,) + tuple(vec_refs) + (gy_ref,), (x_scr, raw0, raw1, raw2, raw3, gy_scr)))]
 
     def q_copies():
         return [pltpu.make_async_copy(q2_scr, q2_out, q_sem.at[0]), pltpu.make_async_copy(d2_scr, d2_out, q_sem.at[1])]
@@ -186,31 +189,37 @@
     barrier = pltpu.get_barrier_semaphore()
     for peer in peers:
         pl.semaphore_signal(barrier, inc=1, device_id={"cp": peer}, device_id_type=pl.DeviceIdType.MESH)
-    for k, ref in enumerate((gain_ref, bias_ref, bq_ref, bv_ref)):
-        vec_scr[k:k + 1, :] = ref[...].astype(F32).reshape(1, width)
     for c in act_copies():
         c.wait()
+    for k, ref in enumerate((raw0, raw1, raw2, raw3)):
+        vec_scr[k:k + 1, :] = ref[...].astype(F32).reshape(1, width)
     normalize(x_scr, vec_scr, x_scr)
 
-    @pl.loop(0, n_pairs)
+    @pl.loop(0, n_pairs // 2)
     def _(i):
-        @pl.when(i < n_pairs - 2)
+        for c in weight_copies(i):
+            c.wait()
+
+        @pl.when(i < n_pairs // 2 - 2)
         def _():
             for c in weight_copies(i + 2):
                 c.start()
-            mem_copy(i).start()
-
-        for c in weight_copies(i):
-            c.wait()
-        block, r = wo_rows(i)
-        q = (dot(x_scr[...], m_scr[wq_at:wo_at, :, cols(i)].reshape(width, PAIR), NN) + pair_of(vec_scr, 2, i)).astype(BF16)
-        d = dot(gy_scr[...], m_scr[wo_at + block, r, :], NT).astype(BF16)
-        q2, d2 = split_heads(q.astype(F32), n_seq), split_heads(d.astype(F32), n_seq)
-        q2_scr[i] = q2
-        d2_scr[i] = d2
-        place(zg_scr, 0, i, q2, lambda j, step: wk_scr[j:j + step, cols(i)])
-        place(zg_scr, 1, i, d2, lambda j, step: wv_scr[j:j + step, cols(i)])
-        ps_scr[i] = dot(d2, jnp.broadcast_to(pair_of(vec_scr, 3, i).astype(BF16), (PAIR, PAIR)), NT)
+
+        @pl.when(i < n_pairs // 2 - 1)
+        def _():
+            mem_copy(2 * i).start()
+            mem_copy(2 * i + 1).start()
+
+        q = (dot(x_scr[...], m_scr[wq_at:wo_at, :, wide(i)].reshape(width, 2 * PAIR), NN) + vec_scr[2:3, wide(i)]).astype(BF16)
+        d = dot(gy_scr[...], m_scr[wo_at + i], NT).astype(BF16)
+        for p in range(2):
+            k = 2 * i + p
+            q2, d2 = (split_heads(t[:, p * PAIR:(p + 1) * PAIR].astype(F32), n_seq) for t in (q, d))
+            q2_scr[k] = q2
+            d2_scr[k] = d2
+            place(zg_scr, 0, k, q2, lambda j, step: wk_scr[j:j + step, cols(k)])
+            place(zg_scr, 1, k, d2, lambda j, step: wv_scr[j:j + step, cols(k)])
+            ps_scr[k] = dot(d2, jnp.broadcast_to(pair_of(vec_scr, 3, k).astype(BF16), (PAIR, PAIR)), NT)
 
     for g in (n_pairs - 2, n_pairs - 1):
         mem_copy(g).start()
@@ -289,15 +298,14 @@
             mine_oq[k, part] = jnp.where(first, top, bottom)
             theirs_oq[k, part] = jnp.where(first, bottom, top)
 
+    lag = 2
     for h in range(n_part):
-        @pl.loop(h * n_each, (h + 1) * n_each)
-        def _(k):
+        for k in range(h * n_each, (h + 1) * n_each):
             o_and_dq(k)
-
         oq_mate(h).start()
-        if h > 0:
-            add_mate(h - 1)
-            oq_across(h - 1).start()
+        if h >= lag:
+            add_mate(h - lag)
+            oq_across(h - lag).start()
 
     def close_dw(k):
         dw_mate(k).wait()
@@ -309,9 +317,10 @@
         def _():
             dw_mate(k - 1).start()
 
-        @pl.when(k == 2)
-        def _():
-            oq_across(n_part - 1).start()
+        for n in range(lag):
+            @pl.when(k == n + 1)
+            def _():
+                oq_across(n_part - lag + n).start()
 
         @pl.when(k == 5)
         def _():
@@ -328,9 +337,10 @@
         e_scr[k] = jnp.where(first, dwk, dwv)
         dp_scr[k] = jnp.where(first, dwv, dwk)
 
-        @pl.when(k == 1)
-        def _():
-            add_mate(n_part - 1)
+        for n in range(lag):
+            @pl.when(k == n)
+            def _():
+                add_mate(n_part - lag + n)
 
         @pl.when(k >= 4)
         def _():
@@ -389,7 +399,7 @@
 
 def assemble(core, own, got, own2, got2, head, head2, at, acc):
     n, width = own.shape[0], own.shape[1] + PAIR
-    step = next(k for k in (192, 128, 64) if n % k == 0 and at % k == 0)
+    step = next(k for k in (256, 192, 128, 64) if n % k == 0 and at % k == 0)
     block = pl.BlockSpec((step, width - PAIR), lambda i: (i, 0))
     head_block = pl.BlockSpec((step, PAIR), lambda i: (at // step + i, 0))
     out = pl.BlockSpec((step, width), lambda i: (at // step + i, 0))
@@ -451,14 +461,14 @@
         h2, gy2 = hidden.reshape(tokens, width), grad_y.reshape(tokens, width)
         blk = n_seq // n_pairs
         quarter = tokens // 4
-        chunks = [width * 3 // 8, width * 5 // 16, width * 3 // 16, width // 8]
+        chunks = [width // 2, width // 4, width * 3 // 16, width // 16]
         anywhere = pl.BlockSpec(memory_space=pl.ANY)
         vm = lambda dt, *s: pltpu.VMEM(s, dt)
         sems = lambda *n: pltpu.SemaphoreType.DMA(n)
         both = lambda n: [sems(n)] * 2
         pg, *rest = pl.pallas_call(
             functools.partial(fused_kernel, scale, n_cp), name="fused",
-            in_specs=[anywhere] * 7 + [pl.BlockSpec(memory_space=pltpu.VMEM)] * 4,
+            in_specs=[anywhere] * 11,
             out_specs=[anywhere] * 10 + [pl.BlockSpec(memory_space=pltpu.VMEM)],
             out_shape=[jax.ShapeDtypeStruct((n_seq, n_fr, 2 * rows), BF16)]
             + [jax.ShapeDtypeStruct((c, width - PAIR), F32) for c in chunks]
@@ -466,7 +476,7 @@
             + [jax.ShapeDtypeStruct((2, tokens, width), BF16)]
             + [jax.ShapeDtypeStruct((n_pairs, 2 * tokens, PAIR), BF16)] * 2
             + [jax.ShapeDtypeStruct((2, n_pairs, PAIR), F32)],
-            scratch_shapes=[vm(BF16, tokens, width), vm(BF16, tokens, width), vm(F32, 4, width),
+            scratch_shapes=[vm(BF16, tokens, width), vm(BF16, tokens, width)] + [vm(BF16, width)] * 4 + [vm(F32, 4, width),
                             vm(BF16, 2, n_pairs, 2 * tokens, width), vm(BF16, n_seq, n_fr, width),
                             vm(F32, n_pairs, blk * n_fr, rows), vm(F32, n_pairs, blk * n_fr, rows),
                             vm(BF16, width, width), vm(BF16, width, width), vm(F32, n_pairs, 2 * tokens, PAIR),
@@ -477,9 +487,9 @@
                             vm(F32, n_pairs, 2, quarter, PAIR), vm(F32, n_pairs, 2, quarter, PAIR),
                             vm(BF16, n_pairs, 2, tokens, PAIR), vm(F32, n_cp, 2, n_pairs, PAIR),
                             vm(F32, n_pairs, width, PAIR),
-                            sems(2), sems(4, n_pairs), sems(n_pairs), sems(2), sems(4, n_pairs), sems(1), sems(2, n_pairs),
+                            sems(6), sems(4, n_pairs // 2), sems(n_pairs), sems(2), sems(4, n_pairs), sems(1), sems(2, n_pairs),
                             sems(2), vm(BF16, 2, blk, n_fr, 2 * rows)]
-            + [sems(n_cp - 1, 4)] * 2 + both(4) + both(4) + both(4) + both(4) + both(n_pairs) + both(n_cp - 1) + both(1),
+            + [sems(n_cp - 1, 4)] * 2 + both(n_pairs) + both(n_pairs) + both(n_pairs) + both(n_pairs) + both(n_pairs) + both(n_cp - 1) + both(1),
             compiler_params=pltpu.CompilerParams(vmem_limit_bytes=VMEM_LIMIT, collective_id=0, has_side_effects=True),
         )(h2, gy2, w_q.reshape(blk, n_fr, width), w_k, w_v, w_o.reshape(blk, n_fr, width), memory, ln_gain, ln_bias, b_q, b_v)
         chips, (head, head_got, oq, q2, d2, small) = rest[:4], rest[4:]

time: 164 us -> 159 us (0.970)
  starting transfers between devices: 7 us -> 1.92 us
  Pallas kernels: 98.4 us -> 94.3 us
  other arithmetic: 6.4 us -> 8.9 us
    ppermute x13, starting transfers between devices: 7 us -> 1.92 us  [swap(): return lax.ppermute(x, 'cp', [(i, i ^ bit) for i in range(n_cp)])]
    pallas_call x4, Pallas kernels: 15.7 us -> 13.7 us  [assemble(): pl.pallas_call(assemble_kernel, grid=(n // step,), name='assemble', in_sp...]
    pallas_call x1, Pallas kernels: 64 us -> 62 us  [device_step(): pl.pallas_call(functools.partial(fused_kernel, scale, n_cp), name='fused'...]
  transfers between devices with their start and end apart: 13 -> 13, of which waited for: 7 -> 8; matrix products, arithmetic and copies ran while one was open for 11% -> 13% of each run, Pallas kernels for 19% -> 19%
where the time goes in v2:
time: 159 us; the launch traced here: 158 us
  Pallas kernels  94.3 us (59%)
  waiting for transfers between devices  38.5 us (24%)
  matrix products  10.9 us (7%)
  other arithmetic  8.9 us (6%)
  local copies, waits for them, and re-layouts  3.11 us (2%)
  starting transfers between devices  1.92 us (1%)
    pallas_call x1, Pallas kernels, device_step(): pl.pallas_call(functools.partial(fused_kernel, scale, n_cp), name='fused'...  62 us
    ppermute x13, waiting for transfers between devices, swap(): return lax.ppermute(x, 'cp', [(i, i ^ bit) for i in range(n_cp)])  38.5 us
    pallas_call x1, Pallas kernels, device_step(): pl.pallas_call(functools.partial(mem_kernel, n_pairs), grid=(2 * n_pairs,...  18.6 us
    pallas_call x4, Pallas kernels, assemble(): pl.pallas_call(assemble_kernel, grid=(n // step,), name='assemble', in_sp...  13.7 us
    dot_general x4, matrix products, dot(): return lax.dot_general(a, b, dims, preferred_element_type=F32)  10.9 us
  transfers between devices with their start and end apart: 13, of which 8 were waited for; matrix products, arithmetic and copies ran while one was open for 13% of the time, Pallas kernels for 19%

profile of v2, /device:TPU:0, one launch (start us, length us, event | category | flops | bytes accessed | tf_op | source)
XLA Modules:
  0.0 158.3 jit_solution(15163776304951872816)
XLA Ops:
  0.6 62.0 %fused.1 = (bf16[32,256,256]{2,1,0:T(8,128)(2,1)}, f32[512,896]{1,0:T(8,128)}, f32[256,896]{1,0:T(8,128)}, f32[192,896]{1,0:T(8,128)}, f32[64,896]{1,0:T(8,128)}...) custom-call(bf16[256,1024]{1,0:T(8,128)(2,1)} %bitcast.35, ...), custom_call_target="tpu_custom_call" | custom-call | tf_op jit(solution)/shard_map/fused/pallas_call | solution.py:469
  62.7 0.0 copy-start
  62.7 0.0 copy-start.2
  62.7 0.0 collective-permute-start
  62.7 0.0 collective-permute-start.4
  62.8 1.3 convert_reduce_fusion
  64.1 1.3 fusion.4
  65.4 0.1 div.17
  65.5 0.7 convert_element_type.41
  66.2 0.7 convert_element_type.43
  66.8 1.7 %convert_reduce_fusion.1 = f32[1024]{0:T(1024)} fusion(bf16[32,8,1024]{2,1,0:T(8,128)(2,1)} %param.23), kind=kLoop, calls=%fused_computation.22 | loop fusion | flops 523264 | bytes 528384 | tf_op jit(solution)/shard_map/reduce_sum | solution.py:516
  68.6 0.1 rsqrt.13
  68.7 0.7 convert_element_type.37
  69.4 0.0 copy-start.4
  69.4 0.0 copy-start.5
  69.4 3.6 %fusion.17 = (f32[1024]{0:T(1024)}, f32[256]{0:T(256)S(1)}, f32[256]{0:T(256)S(1)}, f32[1024]{0:T(1024)}, f32[256,1024]{1,0:T(8,128)S(1)}) fusion(f32[256]{0:T(256)S(1)} %div.17, f32[256]{0:T(256)S(1)} %rsqrt.13, bf16[32,8,1024]{2,1,0:T(8,128)(2,1)} %param.12, f32[1024]{0:T(1024)S(1)} %convert_element_type.41, bf16[1024,1024]{1,0:T(8,128)(2,1)} %param.16, ...), kind=kOutput, calls=%fused_computation.21 | convolution fusion | flops 539489792 | bytes 4210688 | tf_op jit(solution)/shard_map/dot_general | solution.py:23
  73.0 0.0 copy-done
  73.0 0.0 copy-done.2
  73.0 1.3 fusion.16
  74.3 0.0 copy-done.4
  74.3 0.0 copy-done.5
  74.3 1.5 fusion.1
  75.8 2.8 %fusion.24 = f32[1024,1024]{1,0:T(8,128)} fusion(bf16[2,256,1024]{2,1,0:T(8,128)(2,1)S(1)} %copy-done.5, bf16[32,8,1024]{2,1,0:T(8,128)(2,1)S(1)} %copy-done.2), kind=kOutput, calls=%fused_computation.29 | convolution fusion | flops 536870912 | bytes 5242880 | tf_op jit(solution)/shard_map/dot_general | solution.py:23
  78.6 2.9 %fusion.19 = f32[1024,1024]{1,0:T(8,128)} fusion(bf16[32,8,1024]{2,1,0:T(8,128)(2,1)S(1)} %copy-done, f32[1024]{0:T(1024)S(1)} %convert_element_type.43, f32[1024]{0:T(1024)S(1)} %convert_element_type.41, f32[32,8]{1,0:T(8,128)S(1)} %add_rsqrt_fusion, f32[32,8]{1,0:T(8,128)S(1)} %broadcast_multiply_fusion, bf16[2,256,1024]{2,1,0:T(8,128)(2,1)S(1)} %copy-done.5), kind=kOutput, calls=%fused_computation.25 | convolution fusion | flops 538443776 | bytes 5283840 | tf_op jit(solution)/shard_map/dot_general | solution.py:23
  81.5 18.6 %mem.1 = bf16[32,256,1024]{2,1,0:T(8,128)(2,1)} custom-call(bf16[8,512,128]{2,1,0:T(8,128)(2,1)} %get-tuple-element.51.q2_ref, bf16[8,512,128]{2,1,0:T(8,128)(2,1)} %get-tuple-element.52.d2_ref, bf16[1024,1024]{1,0:T(8,128)(2,1)} %wk_ref.3, bf16[1024,1024]{1,0:T(8,128)(2,1)} %wv_ref.3, bf16[32,256,256]{2,1,0:T(8,128)(2,1)} %get-tuple-element.53.pg_ref), custom_call_target="tpu_custom_call" | custom-call | flops 8589934592 | bytes 41943040 | tf_op jit(solution)/shard_map/mem/pallas_call | solution.py:528
  100.1 4.6 %collective-permute-done.got_ref = f32[512,896]{1,0:T(8,128)} collective-permute-done((f32[512,896]{1,0:T(8,128)}, f32[512,896]{1,0:T(8,128)}, u32[]{:S(2)}, u32[]{:S(2)}) %collective-permute-start) | collective-permute-done | bytes 1835040 | tf_op jit(solution)/shard_map/ppermute | solution.py:450
  104.8 0.0 collective-permute-start.5
  104.8 0.3 collective-permute-start.3
  105.0 1.3 add.52.head_ref
  106.3 0.0 copy-start.1
  106.3 0.8 copy-done.1
  107.1 0.2 collective-permute-start.6
  107.3 0.3 collective-permute-start.7
  107.6 1.9 %collective-permute-done.6.head2_ref = f32[1024,128]{1,0:T(8,128)S(1)} collective-permute-done((f32[1024,128]{1,0:T(8,128)S(1)}, f32[1024,128]{1,0:T(8,128)S(1)}, u32[]{:S(2)}, u32[]{:S(2)}) %collective-permute-start.6) | collective-permute-done | bytes 524320 | tf_op jit(solution)/shard_map/ppermute | solution.py:450
  109.5 0.0 copy-start.3
  109.5 0.8 copy-done.3
  110.3 0.0 collective-permute-done.4.own2_ref
  110.3 0.0 collective-permute-done.5.got2_ref
  110.3 4.8 %assemble.4 = (f32[1024,1024]{1,0:T(8,128)}, f32[1024,1024]{1,0:T(8,128)}) custom-call(s32[1]{0:T(128)} %bitcast.10.core_ref, f32[512,896]{1,0:T(8,128)} %get-tuple-element.49.own_ref, f32[512,896]{1,0:T(8,128)} %collective-permute-done.got_ref, f32[512,896]{1,0:T(8,128)} %collective-permute-done.4.own2_ref, f32[512,896]{1,0:T(8,128)} %collective-permute-done.5.got2_ref, ...), custom_call_target="tpu_custom_call" | custom-call | tf_op jit(solution)/shard_map/assemble/pallas_call | solution.py:406
  115.2 12.7 %collective-permute-done.3.got_ref = f32[256,896]{1,0:T(8,128)} collective-permute-done((f32[256,896]{1,0:T(8,128)}, f32[256,896]{1,0:T(8,128)}, u32[]{:S(2)}, u32[]{:S(2)}) %collective-permute-start.3) | collective-permute-done | bytes 917536 | tf_op jit(solution)/shard_map/ppermute | solution.py:450
  127.8 0.0 collective-permute-start.8
  127.8 0.3 collective-permute-start.2
  128.1 0.2 collective-permute-start.9
  128.4 0.0 collective-permute-done.7.own2_ref
  128.4 2.3 %collective-permute-done.8.got2_ref = f32[256,896]{1,0:T(8,128)} collective-permute-done((f32[256,896]{1,0:T(8,128)}, f32[256,896]{1,0:T(8,128)}, u32[]{:S(2)}, u32[]{:S(2)}) %collective-permute-start.8) | collective-permute-done | bytes 917536 | tf_op jit(solution)/shard_map/ppermute | solution.py:450
  130.7 3.7 %assemble.5 = (f32[1024,1024]{1,0:T(8,128)}, f32[1024,1024]{1,0:T(8,128)}) custom-call(s32[1]{0:T(128)} %bitcast.10.core_ref, f32[256,896]{1,0:T(8,128)} %get-tuple-element.63.own_ref, f32[256,896]{1,0:T(8,128)} %collective-permute-done.3.got_ref, f32[256,896]{1,0:T(8,128)} %collective-permute-done.7.own2_ref, ...), custom_call_target="tpu_custom_call", output_to_operand_aliasing={{0}: (7, {}), {1}: (8, {})} | custom-call | tf_op jit(solution)/shard_map/assemble/pallas_call | solution.py:406
  134.3 11.7 %collective-permute-done.2.got_ref = f32[192,896]{1,0:T(8,128)} collective-permute-done((f32[192,896]{1,0:T(8,128)}, f32[192,896]{1,0:T(8,128)}, u32[]{:S(2)}, u32[]{:S(2)}) %collective-permute-start.2) | collective-permute-done | bytes 688160 | tf_op jit(solution)/shard_map/ppermute | solution.py:450
  146.0 0.0 collective-permute-start.10
  146.0 0.3 collective-permute-start.1
  146.3 0.2 collective-permute-start.11
  146.5 0.0 collective-permute-done.9.own2_ref
  146.5 2.0 %collective-permute-done.10.got2_ref = f32[192,896]{1,0:T(8,128)} collective-permute-done((f32[192,896]{1,0:T(8,128)}, f32[192,896]{1,0:T(8,128)}, u32[]{:S(2)}, u32[]{:S(2)}) %collective-permute-start.10) | collective-permute-done | bytes 688160 | tf_op jit(solution)/shard_map/ppermute | solution.py:450
  148.5 3.1 %assemble.6 = (f32[1024,1024]{1,0:T(8,128)}, f32[1024,1024]{1,0:T(8,128)}) custom-call(s32[1]{0:T(128)} %bitcast.10.core_ref, f32[192,896]{1,0:T(8,128)} %get-tuple-element.62.own_ref, f32[192,896]{1,0:T(8,128)} %collective-permute-done.2.got_ref, f32[192,896]{1,0:T(8,128)} %collective-permute-done.9.own2_ref, ...), custom_call_target="tpu_custom_call", output_to_operand_aliasing={{0}: (7, {}), {1}: (8, {})} | custom-call | tf_op jit(solution)/shard_map/assemble/pallas_call | solution.py:406
  151.6 2.8 %collective-permute-done.1.got_ref = f32[64,896]{1,0:T(8,128)} collective-permute-done((f32[64,896]{1,0:T(8,128)}, f32[64,896]{1,0:T(8,128)}, u32[]{:S(2)}, u32[]{:S(2)}) %collective-permute-start.1) | collective-permute-done | bytes 229408 | tf_op jit(solution)/shard_map/ppermute | solution.py:450
  154.3 0.0 collective-permute-start.12
  154.3 1.3 slice_bitcast_fusion
  155.6 0.0 collective-permute-done.11.own2_ref
  155.6 0.5 collective-permute-done.12.got2_ref
  156.2 2.1 %assemble.7 = (f32[1024,1024]{1,0:T(8,128)}, f32[1024,1024]{1,0:T(8,128)}) custom-call(s32[1]{0:T(128)} %bitcast.10.core_ref, f32[64,896]{1,0:T(8,128)} %get-tuple-element.61.own_ref, f32[64,896]{1,0:T(8,128)} %collective-permute-done.1.got_ref, f32[64,896]{1,0:T(8,128)} %collective-permute-done.11.own2_ref, ...), custom_call_target="tpu_custom_call", output_to_operand_aliasing={{0}: (7, {}), {1}: (8, {})} | custom-call | tf_op jit(solution)/shard_map/assemble/pallas_call | solution.py:406
  (3 shorter events, 0.0 us)
Async XLA Ops:
  62.7 10.3 %copy-start = (bf16[32,8,1024]{2,1,0:T(8,128)(2,1)S(1)}, bf16[32,8,1024]{2,1,0:T(8,128)(2,1)}, u32[]{:S(2)}) copy-start(bf16[32,8,1024]{2,1,0:T(8,128)(2,1)} %param.12) | copy-start | bytes 1572868
  62.7 10.3 %copy-start.2 = (bf16[32,8,1024]{2,1,0:T(8,128)(2,1)S(1)}, bf16[32,8,1024]{2,1,0:T(8,128)(2,1)}, u32[]{:S(2)}) copy-start(bf16[32,8,1024]{2,1,0:T(8,128)(2,1)} %param.23) | copy-start | bytes 1572868
  62.7 42.1 %collective-permute-start = (f32[512,896]{1,0:T(8,128)}, f32[512,896]{1,0:T(8,128)}, u32[]{:S(2)}, u32[]{:S(2)}) collective-permute-start(f32[512,896]{1,0:T(8,128)} %get-tuple-element.49.own_ref), channel_id=1, source_target_pairs={{0,2},{1,3},{2,0},{3,1},{4,6},{5,7},{6,4},{7,5},{8,10},{9,11},{10,... | collective-permute-start | bytes 5505032 | tf_op jit(solution)/shard_map/ppermute | solution.py:450
  62.7 47.6 %collective-permute-start.4 = (f32[512,896]{1,0:T(8,128)}, f32[512,896]{1,0:T(8,128)}, u32[]{:S(2)}, u32[]{:S(2)}) collective-permute-start(f32[512,896]{1,0:T(8,128)} %get-tuple-element.49.own_ref), channel_id=1, source_target_pairs={{0,1},{1,0},{2,3},{3,2},{4,5},{5,4},{6,7},{7,6},{8,9},{9,8},{10,11... | collective-permute-start | bytes 5505032 | tf_op jit(solution)/shard_map/ppermute | solution.py:450
  69.4 4.9 %copy-start.4 = (bf16[1024,1024]{1,0:T(8,128)(2,1)S(1)}, bf16[1024,1024]{1,0:T(8,128)(2,1)}, u32[]{:S(2)}) copy-start(bf16[1024,1024]{1,0:T(8,128)(2,1)} %param.21) | copy-start | bytes 6291460
  69.4 4.9 %copy-start.5 = (bf16[2,256,1024]{2,1,0:T(8,128)(2,1)S(1)}, bf16[2,256,1024]{2,1,0:T(8,128)(2,1)}, u32[]{:S(2)}) copy-start(bf16[2,256,1024]{2,1,0:T(8,128)(2,1)} %get-tuple-element.50) | copy-start | bytes 3145732
  104.8 5.6 %collective-permute-start.5 = (f32[512,896]{1,0:T(8,128)}, f32[512,896]{1,0:T(8,128)}, u32[]{:S(2)}, u32[]{:S(2)}) collective-permute-start(f32[512,896]{1,0:T(8,128)} %collective-permute-done.got_ref), channel_id=1, source_target_pairs={{0,1},{1,0},{2,3},{3,2},{4,5},{5,4},{6,7},{7,6},{8,9},{9,8},{10,11... | collective-permute-start | bytes 5505032 | tf_op jit(solution)/shard_map/ppermute | solution.py:450
  104.8 23.1 %collective-permute-start.3 = (f32[256,896]{1,0:T(8,128)}, f32[256,896]{1,0:T(8,128)}, u32[]{:S(2)}, u32[]{:S(2)}) collective-permute-start(f32[256,896]{1,0:T(8,128)} %get-tuple-element.63.own_ref), channel_id=1, source_target_pairs={{0,2},{1,3},{2,0},{3,1},{4,6},{5,7},{6,4},{7,5},{8,10},{9,11},{10,... | collective-permute-start | bytes 2752520 | tf_op jit(solution)/shard_map/ppermute | solution.py:450
  106.3 0.8 copy-start.1
  107.1 2.4 %collective-permute-start.6 = (f32[1024,128]{1,0:T(8,128)S(1)}, f32[1024,128]{1,0:T(8,128)S(1)}, u32[]{:S(2)}, u32[]{:S(2)}) collective-permute-start(f32[1024,128]{1,0:T(8,128)S(1)} %add.52.head_ref), channel_id=1, source_target_pairs={{0,1},{1,0},{2,3},{3,2},{4,5},{5,4},{6,7},{7,6},{8,9},{9,8},{10,11... | collective-permute-start | bytes 1572872 | tf_op jit(solution)/shard_map/ppermute | solution.py:450
  107.3 21.0 %collective-permute-start.7 = (f32[256,896]{1,0:T(8,128)}, f32[256,896]{1,0:T(8,128)}, u32[]{:S(2)}, u32[]{:S(2)}) collective-permute-start(f32[256,896]{1,0:T(8,128)} %get-tuple-element.63.own_ref), channel_id=1, source_target_pairs={{0,1},{1,0},{2,3},{3,2},{4,5},{5,4},{6,7},{7,6},{8,9},{9,8},{10,11... | collective-permute-start | bytes 2752520 | tf_op jit(solution)/shard_map/ppermute | solution.py:450
  109.5 0.8 copy-start.3
  127.8 2.8 %collective-permute-start.8 = (f32[256,896]{1,0:T(8,128)}, f32[256,896]{1,0:T(8,128)}, u32[]{:S(2)}, u32[]{:S(2)}) collective-permute-start(f32[256,896]{1,0:T(8,128)} %collective-permute-done.3.got_ref), channel_id=1, source_target_pairs={{0,1},{1,0},{2,3},{3,2},{4,5},{5,4},{6,7},{7,6},{8,9},{9,8},{10,11... | collective-permute-start | bytes 2752520 | tf_op jit(solution)/shard_map/ppermute | solution.py:450
  127.8 18.2 %collective-permute-start.2 = (f32[192,896]{1,0:T(8,128)}, f32[192,896]{1,0:T(8,128)}, u32[]{:S(2)}, u32[]{:S(2)}) collective-permute-start(f32[192,896]{1,0:T(8,128)} %get-tuple-element.62.own_ref), channel_id=1, source_target_pairs={{0,2},{1,3},{2,0},{3,1},{4,6},{5,7},{6,4},{7,5},{8,10},{9,11},{10,... | collective-permute-start | bytes 2064392 | tf_op jit(solution)/shard_map/ppermute | solution.py:450
  128.1 18.4 %collective-permute-start.9 = (f32[192,896]{1,0:T(8,128)}, f32[192,896]{1,0:T(8,128)}, u32[]{:S(2)}, u32[]{:S(2)}) collective-permute-start(f32[192,896]{1,0:T(8,128)} %get-tuple-element.62.own_ref), channel_id=1, source_target_pairs={{0,1},{1,0},{2,3},{3,2},{4,5},{5,4},{6,7},{7,6},{8,9},{9,8},{10,11... | collective-permute-start | bytes 2064392 | tf_op jit(solution)/shard_map/ppermute | solution.py:450
  146.0 2.5 %collective-permute-start.10 = (f32[192,896]{1,0:T(8,128)}, f32[192,896]{1,0:T(8,128)}, u32[]{:S(2)}, u32[]{:S(2)}) collective-permute-start(f32[192,896]{1,0:T(8,128)} %collective-permute-done.2.got_ref), channel_id=1, source_target_pairs={{0,1},{1,0},{2,3},{3,2},{4,5},{5,4},{6,7},{7,6},{8,9},{9,8},{10,11... | collective-permute-start | bytes 2064392 | tf_op jit(solution)/shard_map/ppermute | solution.py:450
  146.0 8.3 %collective-permute-start.1 = (f32[64,896]{1,0:T(8,128)}, f32[64,896]{1,0:T(8,128)}, u32[]{:S(2)}, u32[]{:S(2)}) collective-permute-start(f32[64,896]{1,0:T(8,128)} %get-tuple-element.61.own_ref), channel_id=1, source_target_pairs={{0,2},{1,3},{2,0},{3,1},{4,6},{5,7},{6,4},{7,5},{8,10},{9,11},{10,... | collective-permute-start | bytes 688136 | tf_op jit(solution)/shard_map/ppermute | solution.py:450
  146.3 9.3 %collective-permute-start.11 = (f32[64,896]{1,0:T(8,128)}, f32[64,896]{1,0:T(8,128)}, u32[]{:S(2)}, u32[]{:S(2)}) collective-permute-start(f32[64,896]{1,0:T(8,128)} %get-tuple-element.61.own_ref), channel_id=1, source_target_pairs={{0,1},{1,0},{2,3},{3,2},{4,5},{5,4},{6,7},{7,6},{8,9},{9,8},{10,11... | collective-permute-start | bytes 688136 | tf_op jit(solution)/shard_map/ppermute | solution.py:450
  154.3 1.8 %collective-permute-start.12 = (f32[64,896]{1,0:T(8,128)}, f32[64,896]{1,0:T(8,128)}, u32[]{:S(2)}, u32[]{:S(2)}) collective-permute-start(f32[64,896]{1,0:T(8,128)} %collective-permute-done.1.got_ref), channel_id=1, source_target_pairs={{0,1},{1,0},{2,3},{3,2},{4,5},{5,4},{6,7},{7,6},{8,9},{9,8},{10,11... | collective-permute-start | bytes 688136 | tf_op jit(solution)/shard_map/ppermute | solution.py:450

commit v3 on v2

--- a/solution.py
+++ b/solution.py
@@ -68,7 +68,7 @@
 def fused_body(scale, n_cp, h_ref, gy_ref, wq_ref, wk_ref, wv_ref, wo_ref, m_ref, vec_refs,
                  pg_ref, chip0_ref, chip1_ref, chip2_ref, chip3_ref, head_ref, head_got, oq_ref, q2_out, d2_out, small_ref,
                  x_scr, gy_scr, raw0, raw1, raw2, raw3, vec_scr, zg_scr, m_scr, e_scr, dp_scr, wk_scr, wv_scr, ps_scr, q2_scr, d2_scr, st_scr, other,
-                 mine_oq, theirs_oq, got_oq, keep_x, give_x, got_x, full_oq, small_scr, got_dw,
+                 part_oq, got_oq, keep_x, give_x, got_x, full_oq, small_scr, got_dw,
                  in_sem, w_sem, m_sem, q_sem, chip_sem, head_sem, out_sem, pg_sem, pg_scr,
                  st_s, st_r, rd_s, rd_r, rx_s, rx_r, ax_s, ax_r, ad_s, ad_r, dw_s, dw_r, sm_s, sm_r, xd_s, xd_r):
     _, n_pairs, n_rows, width = zg_scr.shape
@@ -76,10 +76,9 @@
     n_row = n_rows // n_seq
     rows = n_row * n_pairs
     n_blk = n_seq // n_pairs
-    quarter = keep_x.shape[2]
-    n_part = rd_s.shape[0]
-    n_each = n_pairs // n_part
-    halves = [slice(h * n_each, (h + 1) * n_each) for h in range(n_part)]
+    share = keep_x.shape[3]
+    group = 2 * share
+    grp_seq = n_seq // st_scr.shape[0]
     n_grp = st_scr.shape[0]
     per_grp = n_pairs // n_grp
     me = lax.axis_index("cp")
@@ -145,19 +144,23 @@
             src_ref=st_scr.at[q], dst_ref=other.at[k, q], send_sem=st_s.at[k, q], recv_sem=st_r.at[k, q],
             device_id={"cp": peers[k]}, device_id_type=pl.DeviceIdType.MESH) for k in range(n_cp - 1)]
 
-    def oq_mate(h):
-        return send(theirs_oq.at[halves[h]], got_oq.at[halves[h]], (rd_s, rd_r), h, mate)
-
-    def oq_across(h):
-        return send(give_x.at[halves[h]], got_x.at[halves[h]], (rx_s, rx_r), h, across)
-
-    def own_across(h):
-        at = pl.ds(pl.multiple_of((2 * core + chip) * quarter, quarter), quarter)
-        return send(full_oq.at[halves[h], :, at, :], full_oq.at[halves[h], :, at, :], (ax_s, ax_r), h, across)
-
-    def half_mate(h):
-        at = pl.ds(pl.multiple_of(core * 2 * quarter, quarter), 2 * quarter)
-        return send(full_oq.at[halves[h], :, at, :], full_oq.at[halves[h], :, at, :], (ad_s, ad_r), h, mate)
+    def oq_mate(g):
+        j = lax.rem(g, 2)
+        return send(part_oq.at[g], got_oq.at[j], (rd_s, rd_r), j, mate)
+
+    def oq_across(j):
+        return send(give_x.at[j], got_x.at[j], (rx_s, rx_r), j, across)
+
+    def own_rows(j):
+        return pl.ds(pl.multiple_of((2 * core + j) * group + chip * share, share), share)
+
+    def own_across(j):
+        at = own_rows(j)
+        return send(full_oq.at[:, :, at, :], full_oq.at[:, :, at, :], (ax_s, ax_r), j, across)
+
+    def group_mate(j):
+        at = pl.ds(pl.multiple_of((2 * core + j) * group, group), group)
+        return send(full_oq.at[:, :, at, :], full_oq.at[:, :, at, :], (ad_s, ad_r), j, mate)
 
     def dw_mate(k):
         return send(dp_scr.at[k], got_dw.at[k], (dw_s, dw_r), k, mate)
@@ -165,26 +168,29 @@
     def small_copy(k):
         return send(small_scr.at[me], small_scr.at[me], (sm_s, sm_r), k, peers[k])
 
-    def add_mate(h):
-        oq_mate(h).wait()
-        t = mine_oq[halves[h]] + got_oq[halves[h]]
-        top, bottom = t[:, :, :quarter], t[:, :, quarter:]
-        keep_x[halves[h]] = jnp.where(left, top, bottom)
-        give_x[halves[h]] = jnp.where(left, bottom, top)
-
-    def finish(h):
-        oq_across(h).wait()
-        t = keep_x[halves[h]] + got_x[halves[h]]
-        at = pl.ds(pl.multiple_of((2 * core + chip) * quarter, quarter), quarter)
-        full_oq[halves[h], :, at, :] = t.astype(BF16)
-        small_scr[me, 0, halves[h], :] = jnp.sum(t[:, 1], axis=1)
+    def take_group(g):
+        @pl.when(core == lax.div(g, 2))
+        def _():
+            j = lax.rem(g, 2)
+            oq_mate(g).wait_recv()
+            t = part_oq[g] + got_oq[j]
+            top, bottom = t[:, :, :share], t[:, :, share:]
+            keep_x[j] = jnp.where(left, top, bottom)
+            give_x[j] = jnp.where(left, bottom, top)
+            oq_across(j).start()
+
+    def finish(j):
+        oq_across(j).wait()
+        t = keep_x[j] + got_x[j]
+        full_oq[:, :, own_rows(j), :] = t.astype(BF16)
+        total = jnp.sum(t[:, 1], axis=1)
+        small_scr[me, 0] = total if j == 0 else small_scr[me, 0] + total
 
     for c in act_copies():
         c.start()
 
-    for k in range(2):
-        for c in weight_copies(k):
-            c.start()
+    for c in weight_copies(0):
+        c.start()
 
     barrier = pltpu.get_barrier_semaphore()
     for peer in peers:
@@ -197,13 +203,13 @@
 
     @pl.loop(0, n_pairs // 2)
     def _(i):
+        @pl.when(i < n_pairs // 2 - 1)
+        def _():
+            for c in weight_copies(i + 1):
+                c.start()
+
         for c in weight_copies(i):
             c.wait()
-
-        @pl.when(i < n_pairs // 2 - 2)
-        def _():
-            for c in weight_copies(i + 2):
-                c.start()
 
         @pl.when(i < n_pairs // 2 - 1)
         def _():
@@ -228,84 +234,79 @@
 
     pl.semaphore_wait(barrier, n_cp - 1)
 
-    @pl.loop(0, n_pairs)
-    def _(g):
-        grp = lax.div(g, per_grp)
-
-        @pl.when((g > 0) & (lax.rem(g, per_grp) == 0))
+    @pl.loop(0, n_grp)
+    def _(grp):
+        @pl.when(grp > 0)
         def _():
             for c in stats_copies(grp - 1):
                 c.start()
 
-        mem_copy(g).wait()
-        for j in range(n_blk):
-            b = g * n_blk + j
-            at = pl.ds(lax.rem(g, per_grp) * n_blk + j, 1)
+        for n in range(per_grp):
+            mem_copy(grp * per_grp + n).wait()
+        for j in range(per_grp * n_blk):
+            g, r0 = grp * per_grp + j // n_blk, j % n_blk * n_fr
+            b = grp * per_grp * n_blk + j
             t = dot(m_scr[b], zg_scr[:, :, seq_rows(b), :].reshape(2 * rows, width), NT)
             s = t[:, :rows] * scale
             dp = t[:, rows:] + ps_scr[:, seq_rows(b), :].reshape(rows, PAIR).T[0:1, :]
             mx = jnp.max(s, axis=0, keepdims=True)
             e = jnp.exp(s - mx)
-            e_scr[g, j * n_fr:(j + 1) * n_fr, :] = e
-            dp_scr[g, j * n_fr:(j + 1) * n_fr, :] = dp
-            st_scr[grp, 0, at, :] = mx
-            st_scr[grp, 1, at, :] = jnp.sum(e, axis=0, keepdims=True)
-            st_scr[grp, 2, at, :] = jnp.sum(e * dp, axis=0, keepdims=True)
+            e_scr[g, r0:r0 + n_fr, :] = e
+            dp_scr[g, r0:r0 + n_fr, :] = dp
+            st_scr[grp, 0, j:j + 1, :] = mx
+            st_scr[grp, 1, j:j + 1, :] = jnp.sum(e, axis=0, keepdims=True)
+            st_scr[grp, 2, j:j + 1, :] = jnp.sum(e * dp, axis=0, keepdims=True)
 
     for c in stats_copies(n_grp - 1):
         c.start()
 
-    @pl.loop(0, n_pairs)
-    def _(g):
-        grp = lax.div(g, per_grp)
-
-        @pl.when(lax.rem(g, per_grp) == 0)
-        def _():
-            for c in stats_copies(grp):
-                c.wait()
-
-        @pl.when(g >= 2)
-        def _():
-            pg_copy(g - 2).wait()
-
-        slot = lax.rem(g, 2)
+    @pl.loop(0, n_grp)
+    def _(grp):
+        for c in stats_copies(grp):
+            c.wait()
+
+        @pl.when(grp > 0)
+        def _():
+            for n in range(per_grp):
+                pg_copy((grp - 1) * per_grp + n).wait()
+
         ones = jnp.ones((n_fr, PAIR), BF16)
-        for j in range(n_blk):
-            b = g * n_blk + j
-            at = pl.ds(lax.rem(g, per_grp) * n_blk + j, 1)
-            tops, sums_l, sums_c = ([st_scr[grp, n, at, :]] + [other[k, grp, n, at, :] for k in range(n_cp - 1)] for n in range(3))
+        for j in range(per_grp * n_blk):
+            g, r0 = grp * per_grp + j // n_blk, j % n_blk * n_fr
+            b = grp * per_grp * n_blk + j
+            tops, sums_l, sums_c = ([st_scr[grp, n, j:j + 1, :]] + [other[k, grp, n, j:j + 1, :] for k in range(n_cp - 1)]
+                                    for n in range(3))
             top = functools.reduce(jnp.maximum, tops)
             fac = [jnp.exp(t - top) for t in tops]
             total = functools.reduce(jnp.add, [f * v for f, v in zip(fac, sums_l)])
             c = functools.reduce(jnp.add, [f * v for f, v in zip(fac, sums_c)]) / total
-            p = e_scr[g, j * n_fr:(j + 1) * n_fr, :] * (fac[0] / total)
-            gr = p * (dp_scr[g, j * n_fr:(j + 1) * n_fr, :] - c) * scale
+            p = e_scr[g, r0:r0 + n_fr, :] * (fac[0] / total)
+            gr = p * (dp_scr[g, r0:r0 + n_fr, :] - c) * scale
             pg = jnp.concatenate([gr.astype(BF16), p.astype(BF16)], axis=1)
-            pg_scr[slot, j] = pg
+            pg_scr[j // n_blk, j % n_blk] = pg
             pgt = pg.T
             step = 256
             for w in range(0, width, step):
                 t = dot(pgt, m_scr[b, :, w:w + step], NN).astype(BF16)
                 zg_scr[:, :, seq_rows(b), w:w + step] = t.reshape(2, n_pairs, n_row, step)
             ps_scr[:, seq_rows(b), :] = dot(pgt[rows:], ones, NN).reshape(n_pairs, n_row, PAIR)
-        pg_copy(g).start()
-
-    def o_and_dq(k):
-        o = join_heads(dot(zg_scr[1, k], wv_scr[:, cols(k)], NN), n_seq) + join_heads(ps_scr[k], n_seq) * pair_of(vec_scr, 3, k)
-        dq = join_heads(dot(zg_scr[0, k], wk_scr[:, cols(k)], NN), n_seq)
-        for part, t in enumerate((o, dq)):
-            top, bottom = t[:t.shape[0] // 2], t[t.shape[0] // 2:]
-            mine_oq[k, part] = jnp.where(first, top, bottom)
-            theirs_oq[k, part] = jnp.where(first, bottom, top)
-
-    lag = 2
-    for h in range(n_part):
-        for k in range(h * n_each, (h + 1) * n_each):
-            o_and_dq(k)
-        oq_mate(h).start()
-        if h >= lag:
-            add_mate(h - lag)
-            oq_across(h - lag).start()
+        for n in range(per_grp):
+            pg_copy(grp * per_grp + n).start()
+
+        @pl.when(grp > 0)
+        def _():
+            take_group(grp - 1)
+
+        at = pl.ds(pl.multiple_of(grp * (grp_seq * n_row), grp_seq * n_row), grp_seq * n_row)
+        for k in range(n_pairs):
+            c = slice(k * PAIR, (k + 1) * PAIR)
+            sums = join_heads(ps_scr[k, at, :], grp_seq)
+            part_oq[grp, k, 0] = join_heads(dot(zg_scr[1, k, at, :], wv_scr[:, c], NN), grp_seq) + sums * vec_scr[3:4, c]
+            part_oq[grp, k, 1] = join_heads(dot(zg_scr[0, k, at, :], wk_scr[:, c], NN), grp_seq)
+
+        @pl.when(core != lax.div(grp, 2))
+        def _():
+            oq_mate(grp).start()
 
     def close_dw(k):
         dw_mate(k).wait()
@@ -316,11 +317,6 @@
         @pl.when(k >= 1)
         def _():
             dw_mate(k - 1).start()
-
-        for n in range(lag):
-            @pl.when(k == n + 1)
-            def _():
-                oq_across(n_part - lag + n).start()
 
         @pl.when(k == 5)
         def _():
@@ -337,10 +333,9 @@
         e_scr[k] = jnp.where(first, dwk, dwv)
         dp_scr[k] = jnp.where(first, dwv, dwk)
 
-        for n in range(lag):
-            @pl.when(k == n)
-            def _():
-                add_mate(n_part - lag + n)
+        @pl.when(k == 2)
+        def _():
+            take_group(n_grp - 1)
 
         @pl.when(k >= 4)
         def _():
@@ -357,20 +352,21 @@
         for c in chip_copies(k):
             c.start()
 
-    for h in range(n_part):
-        finish(h)
-        own_across(h).start()
+    for j in range(2):
+        finish(j)
+        own_across(j).start()
     for k in range(n_cp - 1):
         small_copy(k).start()
     head_across().start()
-    for h in range(n_part):
-        own_across(h).wait()
-        half_mate(h).start()
+    for j in range(2):
+        own_across(j).wait()
+        group_mate(j).start()
     for k in range(n_cp - 1):
         small_copy(k).wait()
     small_ref[...] = small_scr[0] + small_scr[1] + small_scr[2] + small_scr[3]
-    for h in range(n_part):
-        half_mate(h).wait()
+    for j in range(2):
+        group_mate(j).wait()
+        oq_mate(2 * (1 - core) + j).wait_send()
     for c in out_copies():
         c.start()
 
@@ -482,14 +478,13 @@
                             vm(BF16, width, width), vm(BF16, width, width), vm(F32, n_pairs, 2 * tokens, PAIR),
                             vm(BF16, n_pairs, 2 * tokens, PAIR), vm(BF16, n_pairs, 2 * tokens, PAIR),
                             vm(F32, 4, 3, n_seq // 4, rows), vm(F32, n_cp - 1, 4, 3, n_seq // 4, rows),
-                            vm(F32, n_pairs, 2, 2 * quarter, PAIR), vm(F32, n_pairs, 2, 2 * quarter, PAIR),
-                            vm(F32, n_pairs, 2, 2 * quarter, PAIR), vm(F32, n_pairs, 2, quarter, PAIR),
-                            vm(F32, n_pairs, 2, quarter, PAIR), vm(F32, n_pairs, 2, quarter, PAIR),
+                            vm(F32, 4, n_pairs, 2, quarter, PAIR), vm(F32, 2, n_pairs, 2, quarter, PAIR)]
+            + [vm(F32, 2, n_pairs, 2, quarter // 2, PAIR)] * 3 + [
                             vm(BF16, n_pairs, 2, tokens, PAIR), vm(F32, n_cp, 2, n_pairs, PAIR),
                             vm(F32, n_pairs, width, PAIR),
                             sems(6), sems(4, n_pairs // 2), sems(n_pairs), sems(2), sems(4, n_pairs), sems(1), sems(2, n_pairs),
                             sems(2), vm(BF16, 2, blk, n_fr, 2 * rows)]
-            + [sems(n_cp - 1, 4)] * 2 + both(n_pairs) + both(n_pairs) + both(n_pairs) + both(n_pairs) + both(n_pairs) + both(n_cp - 1) + both(1),
+            + [sems(n_cp - 1, 4)] * 2 + both(2) + both(2) + both(2) + both(2) + both(n_pairs) + both(n_cp - 1) + both(1),
             compiler_params=pltpu.CompilerParams(vmem_limit_bytes=VMEM_LIMIT, collective_id=0, has_side_effects=True),
         )(h2, gy2, w_q.reshape(blk, n_fr, width), w_k, w_v, w_o.reshape(blk, n_fr, width), memory, ln_gain, ln_bias, b_q, b_v)
         chips, (head, head_got, oq, q2, d2, small) = rest[:4], rest[4:]

time: 159 us -> 156 us (0.981)
  Pallas kernels: 94.3 us -> 91.8 us
    pallas_call x1, Pallas kernels: 62 us -> 59.5 us  [device_step(): pl.pallas_call(functools.partial(fused_kernel, scale, n_cp), name='fused'...]
  transfers between devices with their start and end apart: 13 -> 13, of which waited for: 8 -> 8; matrix products, arithmetic and copies ran while one was open for 13% -> 14% of each run, Pallas kernels for 19% -> 19%
where the time goes in v3:
time: 156 us
  Pallas kernels  91.8 us (59%)
  waiting for transfers between devices  38.2 us (24%)
  matrix products  10.9 us (7%)
  other arithmetic  8.9 us (6%)
  local copies, waits for them, and re-layouts  3.11 us (2%)
  starting transfers between devices  1.92 us (1%)
    pallas_call x1, Pallas kernels, device_step(): pl.pallas_call(functools.partial(fused_kernel, scale, n_cp), name='fused'...  59.5 us
    ppermute x13, waiting for transfers between devices, swap(): return lax.ppermute(x, 'cp', [(i, i ^ bit) for i in range(n_cp)])  38.2 us
    pallas_call x1, Pallas kernels, device_step(): pl.pallas_call(functools.partial(mem_kernel, n_pairs), grid=(2 * n_pairs,...  18.6 us
    pallas_call x4, Pallas kernels, assemble(): pl.pallas_call(assemble_kernel, grid=(n // step,), name='assemble', in_sp...  13.7 us
    dot_general x4, matrix products, dot(): return lax.dot_general(a, b, dims, preferred_element_type=F32)  10.9 us
  transfers between devices with their start and end apart: 13, of which 8 were waited for; matrix products, arithmetic and copies ran while one was open for 14% of the time, Pallas kernels for 19%

profile of v3, /device:TPU:0, one launch (start us, length us, event | category | flops | bytes accessed | tf_op | source)
XLA Modules:
  0.0 155.5 jit_solution(16676780246027563436)
XLA Ops:
  0.6 59.5 %fused.1 = (bf16[32,256,256]{2,1,0:T(8,128)(2,1)}, f32[512,896]{1,0:T(8,128)}, f32[256,896]{1,0:T(8,128)}, f32[192,896]{1,0:T(8,128)}, f32[64,896]{1,0:T(8,128)}...) custom-call(bf16[256,1024]{1,0:T(8,128)(2,1)} %bitcast.35, ...), custom_call_target="tpu_custom_call" | custom-call | tf_op jit(solution)/shard_map/fused/pallas_call | solution.py:465
  60.1 0.0 copy-start
  60.1 0.0 copy-start.2
  60.1 0.0 collective-permute-start
  60.2 0.0 collective-permute-start.4
  60.2 1.3 convert_reduce_fusion
  61.5 1.3 fusion.4
  62.8 0.1 div.17
  62.9 0.7 convert_element_type.41
  63.6 0.7 convert_element_type.43
  64.3 1.7 %convert_reduce_fusion.1 = f32[1024]{0:T(1024)} fusion(bf16[32,8,1024]{2,1,0:T(8,128)(2,1)} %param.23), kind=kLoop, calls=%fused_computation.22 | loop fusion | flops 523264 | bytes 528384 | tf_op jit(solution)/shard_map/reduce_sum | solution.py:511
  66.0 0.1 rsqrt.13
  66.1 0.7 convert_element_type.37
  66.8 0.0 copy-start.4
  66.8 0.0 copy-start.5
  66.8 3.6 %fusion.17 = (f32[1024]{0:T(1024)}, f32[256]{0:T(256)S(1)}, f32[256]{0:T(256)S(1)}, f32[1024]{0:T(1024)}, f32[256,1024]{1,0:T(8,128)S(1)}) fusion(f32[256]{0:T(256)S(1)} %div.17, f32[256]{0:T(256)S(1)} %rsqrt.13, bf16[32,8,1024]{2,1,0:T(8,128)(2,1)} %param.12, f32[1024]{0:T(1024)S(1)} %convert_element_type.41, bf16[1024,1024]{1,0:T(8,128)(2,1)} %param.16, ...), kind=kOutput, calls=%fused_computation.21 | convolution fusion | flops 539489792 | bytes 4210688 | tf_op jit(solution)/shard_map/dot_general | solution.py:23
  70.5 0.0 copy-done
  70.5 0.0 copy-done.2
  70.5 1.3 fusion.16
  71.7 0.0 copy-done.4
  71.7 0.0 copy-done.5
  71.7 1.5 fusion.1
  73.3 2.8 %fusion.24 = f32[1024,1024]{1,0:T(8,128)} fusion(bf16[2,256,1024]{2,1,0:T(8,128)(2,1)S(1)} %copy-done.5, bf16[32,8,1024]{2,1,0:T(8,128)(2,1)S(1)} %copy-done.2), kind=kOutput, calls=%fused_computation.29 | convolution fusion | flops 536870912 | bytes 5242880 | tf_op jit(solution)/shard_map/dot_general | solution.py:23
  76.0 2.9 %fusion.19 = f32[1024,1024]{1,0:T(8,128)} fusion(bf16[32,8,1024]{2,1,0:T(8,128)(2,1)S(1)} %copy-done, f32[1024]{0:T(1024)S(1)} %convert_element_type.43, f32[1024]{0:T(1024)S(1)} %convert_element_type.41, f32[32,8]{1,0:T(8,128)S(1)} %add_rsqrt_fusion, f32[32,8]{1,0:T(8,128)S(1)} %broadcast_multiply_fusion, bf16[2,256,1024]{2,1,0:T(8,128)(2,1)S(1)} %copy-done.5), kind=kOutput, calls=%fused_computation.25 | convolution fusion | flops 538443776 | bytes 5283840 | tf_op jit(solution)/shard_map/dot_general | solution.py:23
  79.0 18.6 %mem.1 = bf16[32,256,1024]{2,1,0:T(8,128)(2,1)} custom-call(bf16[8,512,128]{2,1,0:T(8,128)(2,1)} %get-tuple-element.51.q2_ref, bf16[8,512,128]{2,1,0:T(8,128)(2,1)} %get-tuple-element.52.d2_ref, bf16[1024,1024]{1,0:T(8,128)(2,1)} %wk_ref.3, bf16[1024,1024]{1,0:T(8,128)(2,1)} %wv_ref.3, bf16[32,256,256]{2,1,0:T(8,128)(2,1)} %get-tuple-element.53.pg_ref), custom_call_target="tpu_custom_call" | custom-call | flops 8589934592 | bytes 41943040 | tf_op jit(solution)/shard_map/mem/pallas_call | solution.py:523
  97.6 4.4 %collective-permute-done.got_ref = f32[512,896]{1,0:T(8,128)} collective-permute-done((f32[512,896]{1,0:T(8,128)}, f32[512,896]{1,0:T(8,128)}, u32[]{:S(2)}, u32[]{:S(2)}) %collective-permute-start) | collective-permute-done | bytes 1835040 | tf_op jit(solution)/shard_map/ppermute | solution.py:446
  102.0 0.0 collective-permute-start.5
  102.0 0.3 collective-permute-start.3
  102.3 1.3 add.52.head_ref
  103.5 0.0 copy-start.1
  103.5 0.8 copy-done.1
  104.3 0.2 collective-permute-start.6
  104.6 0.3 collective-permute-start.7
  104.8 1.9 %collective-permute-done.6.head2_ref = f32[1024,128]{1,0:T(8,128)S(1)} collective-permute-done((f32[1024,128]{1,0:T(8,128)S(1)}, f32[1024,128]{1,0:T(8,128)S(1)}, u32[]{:S(2)}, u32[]{:S(2)}) %collective-permute-start.6) | collective-permute-done | bytes 524320 | tf_op jit(solution)/shard_map/ppermute | solution.py:446
  106.7 0.0 copy-start.3
  106.7 0.8 copy-done.3
  107.6 0.0 collective-permute-done.4.own2_ref
  107.6 0.0 collective-permute-done.5.got2_ref
  107.6 4.8 %assemble.4 = (f32[1024,1024]{1,0:T(8,128)}, f32[1024,1024]{1,0:T(8,128)}) custom-call(s32[1]{0:T(128)} %bitcast.10.core_ref, f32[512,896]{1,0:T(8,128)} %get-tuple-element.49.own_ref, f32[512,896]{1,0:T(8,128)} %collective-permute-done.got_ref, f32[512,896]{1,0:T(8,128)} %collective-permute-done.4.own2_ref, f32[512,896]{1,0:T(8,128)} %collective-permute-done.5.got2_ref, ...), custom_call_target="tpu_custom_call" | custom-call | tf_op jit(solution)/shard_map/assemble/pallas_call | solution.py:402
  112.4 12.7 %collective-permute-done.3.got_ref = f32[256,896]{1,0:T(8,128)} collective-permute-done((f32[256,896]{1,0:T(8,128)}, f32[256,896]{1,0:T(8,128)}, u32[]{:S(2)}, u32[]{:S(2)}) %collective-permute-start.3) | collective-permute-done | bytes 917536 | tf_op jit(solution)/shard_map/ppermute | solution.py:446
  125.1 0.0 collective-permute-start.8
  125.1 0.3 collective-permute-start.2
  125.3 0.2 collective-permute-start.9
  125.6 0.0 collective-permute-done.7.own2_ref
  125.6 2.3 %collective-permute-done.8.got2_ref = f32[256,896]{1,0:T(8,128)} collective-permute-done((f32[256,896]{1,0:T(8,128)}, f32[256,896]{1,0:T(8,128)}, u32[]{:S(2)}, u32[]{:S(2)}) %collective-permute-start.8) | collective-permute-done | bytes 917536 | tf_op jit(solution)/shard_map/ppermute | solution.py:446
  127.9 3.7 %assemble.5 = (f32[1024,1024]{1,0:T(8,128)}, f32[1024,1024]{1,0:T(8,128)}) custom-call(s32[1]{0:T(128)} %bitcast.10.core_ref, f32[256,896]{1,0:T(8,128)} %get-tuple-element.63.own_ref, f32[256,896]{1,0:T(8,128)} %collective-permute-done.3.got_ref, f32[256,896]{1,0:T(8,128)} %collective-permute-done.7.own2_ref, ...), custom_call_target="tpu_custom_call", output_to_operand_aliasing={{0}: (7, {}), {1}: (8, {})} | custom-call | tf_op jit(solution)/shard_map/assemble/pallas_call | solution.py:402
  131.5 11.7 %collective-permute-done.2.got_ref = f32[192,896]{1,0:T(8,128)} collective-permute-done((f32[192,896]{1,0:T(8,128)}, f32[192,896]{1,0:T(8,128)}, u32[]{:S(2)}, u32[]{:S(2)}) %collective-permute-start.2) | collective-permute-done | bytes 688160 | tf_op jit(solution)/shard_map/ppermute | solution.py:446
  143.2 0.0 collective-permute-start.10
  143.2 0.3 collective-permute-start.1
  143.5 0.2 collective-permute-start.11
  143.7 0.0 collective-permute-done.9.own2_ref
  143.7 2.0 %collective-permute-done.10.got2_ref = f32[192,896]{1,0:T(8,128)} collective-permute-done((f32[192,896]{1,0:T(8,128)}, f32[192,896]{1,0:T(8,128)}, u32[]{:S(2)}, u32[]{:S(2)}) %collective-permute-start.10) | collective-permute-done | bytes 688160 | tf_op jit(solution)/shard_map/ppermute | solution.py:446
  145.7 3.1 %assemble.6 = (f32[1024,1024]{1,0:T(8,128)}, f32[1024,1024]{1,0:T(8,128)}) custom-call(s32[1]{0:T(128)} %bitcast.10.core_ref, f32[192,896]{1,0:T(8,128)} %get-tuple-element.62.own_ref, f32[192,896]{1,0:T(8,128)} %collective-permute-done.2.got_ref, f32[192,896]{1,0:T(8,128)} %collective-permute-done.9.own2_ref, ...), custom_call_target="tpu_custom_call", output_to_operand_aliasing={{0}: (7, {}), {1}: (8, {})} | custom-call | tf_op jit(solution)/shard_map/assemble/pallas_call | solution.py:402
  148.8 2.8 %collective-permute-done.1.got_ref = f32[64,896]{1,0:T(8,128)} collective-permute-done((f32[64,896]{1,0:T(8,128)}, f32[64,896]{1,0:T(8,128)}, u32[]{:S(2)}, u32[]{:S(2)}) %collective-permute-start.1) | collective-permute-done | bytes 229408 | tf_op jit(solution)/shard_map/ppermute | solution.py:446
  151.6 0.0 collective-permute-start.12
  151.6 1.3 slice_bitcast_fusion
  152.8 0.0 collective-permute-done.11.own2_ref
  152.8 0.5 collective-permute-done.12.got2_ref
  153.4 2.1 %assemble.7 = (f32[1024,1024]{1,0:T(8,128)}, f32[1024,1024]{1,0:T(8,128)}) custom-call(s32[1]{0:T(128)} %bitcast.10.core_ref, f32[64,896]{1,0:T(8,128)} %get-tuple-element.61.own_ref, f32[64,896]{1,0:T(8,128)} %collective-permute-done.1.got_ref, f32[64,896]{1,0:T(8,128)} %collective-permute-done.11.own2_ref, ...), custom_call_target="tpu_custom_call", output_to_operand_aliasing={{0}: (7, {}), {1}: (8, {})} | custom-call | tf_op jit(solution)/shard_map/assemble/pallas_call | solution.py:402
  (3 shorter events, 0.0 us)
Async XLA Ops:
  60.1 10.3 %copy-start = (bf16[32,8,1024]{2,1,0:T(8,128)(2,1)S(1)}, bf16[32,8,1024]{2,1,0:T(8,128)(2,1)}, u32[]{:S(2)}) copy-start(bf16[32,8,1024]{2,1,0:T(8,128)(2,1)} %param.12) | copy-start | bytes 1572868
  60.1 10.3 %copy-start.2 = (bf16[32,8,1024]{2,1,0:T(8,128)(2,1)S(1)}, bf16[32,8,1024]{2,1,0:T(8,128)(2,1)}, u32[]{:S(2)}) copy-start(bf16[32,8,1024]{2,1,0:T(8,128)(2,1)} %param.23) | copy-start | bytes 1572868
  60.1 41.8 %collective-permute-start = (f32[512,896]{1,0:T(8,128)}, f32[512,896]{1,0:T(8,128)}, u32[]{:S(2)}, u32[]{:S(2)}) collective-permute-start(f32[512,896]{1,0:T(8,128)} %get-tuple-element.49.own_ref), channel_id=1, source_target_pairs={{0,2},{1,3},{2,0},{3,1},{4,6},{5,7},{6,4},{7,5},{8,10},{9,11},{10,... | collective-permute-start | bytes 5505032 | tf_op jit(solution)/shard_map/ppermute | solution.py:446
  60.2 47.4 %collective-permute-start.4 = (f32[512,896]{1,0:T(8,128)}, f32[512,896]{1,0:T(8,128)}, u32[]{:S(2)}, u32[]{:S(2)}) collective-permute-start(f32[512,896]{1,0:T(8,128)} %get-tuple-element.49.own_ref), channel_id=1, source_target_pairs={{0,1},{1,0},{2,3},{3,2},{4,5},{5,4},{6,7},{7,6},{8,9},{9,8},{10,11... | collective-permute-start | bytes 5505032 | tf_op jit(solution)/shard_map/ppermute | solution.py:446
  66.8 4.9 %copy-start.4 = (bf16[1024,1024]{1,0:T(8,128)(2,1)S(1)}, bf16[1024,1024]{1,0:T(8,128)(2,1)}, u32[]{:S(2)}) copy-start(bf16[1024,1024]{1,0:T(8,128)(2,1)} %param.21) | copy-start | bytes 6291460
  66.8 4.9 %copy-start.5 = (bf16[2,256,1024]{2,1,0:T(8,128)(2,1)S(1)}, bf16[2,256,1024]{2,1,0:T(8,128)(2,1)}, u32[]{:S(2)}) copy-start(bf16[2,256,1024]{2,1,0:T(8,128)(2,1)} %get-tuple-element.50) | copy-start | bytes 3145732
  102.0 5.6 %collective-permute-start.5 = (f32[512,896]{1,0:T(8,128)}, f32[512,896]{1,0:T(8,128)}, u32[]{:S(2)}, u32[]{:S(2)}) collective-permute-start(f32[512,896]{1,0:T(8,128)} %collective-permute-done.got_ref), channel_id=1, source_target_pairs={{0,1},{1,0},{2,3},{3,2},{4,5},{5,4},{6,7},{7,6},{8,9},{9,8},{10,11... | collective-permute-start | bytes 5505032 | tf_op jit(solution)/shard_map/ppermute | solution.py:446
  102.0 23.1 %collective-permute-start.3 = (f32[256,896]{1,0:T(8,128)}, f32[256,896]{1,0:T(8,128)}, u32[]{:S(2)}, u32[]{:S(2)}) collective-permute-start(f32[256,896]{1,0:T(8,128)} %get-tuple-element.63.own_ref), channel_id=1, source_target_pairs={{0,2},{1,3},{2,0},{3,1},{4,6},{5,7},{6,4},{7,5},{8,10},{9,11},{10,... | collective-permute-start | bytes 2752520 | tf_op jit(solution)/shard_map/ppermute | solution.py:446
  103.5 0.8 copy-start.1
  104.3 2.4 %collective-permute-start.6 = (f32[1024,128]{1,0:T(8,128)S(1)}, f32[1024,128]{1,0:T(8,128)S(1)}, u32[]{:S(2)}, u32[]{:S(2)}) collective-permute-start(f32[1024,128]{1,0:T(8,128)S(1)} %add.52.head_ref), channel_id=1, source_target_pairs={{0,1},{1,0},{2,3},{3,2},{4,5},{5,4},{6,7},{7,6},{8,9},{9,8},{10,11... | collective-permute-start | bytes 1572872 | tf_op jit(solution)/shard_map/ppermute | solution.py:446
  104.6 21.0 %collective-permute-start.7 = (f32[256,896]{1,0:T(8,128)}, f32[256,896]{1,0:T(8,128)}, u32[]{:S(2)}, u32[]{:S(2)}) collective-permute-start(f32[256,896]{1,0:T(8,128)} %get-tuple-element.63.own_ref), channel_id=1, source_target_pairs={{0,1},{1,0},{2,3},{3,2},{4,5},{5,4},{6,7},{7,6},{8,9},{9,8},{10,11... | collective-permute-start | bytes 2752520 | tf_op jit(solution)/shard_map/ppermute | solution.py:446
  106.7 0.8 copy-start.3
  125.1 2.8 %collective-permute-start.8 = (f32[256,896]{1,0:T(8,128)}, f32[256,896]{1,0:T(8,128)}, u32[]{:S(2)}, u32[]{:S(2)}) collective-permute-start(f32[256,896]{1,0:T(8,128)} %collective-permute-done.3.got_ref), channel_id=1, source_target_pairs={{0,1},{1,0},{2,3},{3,2},{4,5},{5,4},{6,7},{7,6},{8,9},{9,8},{10,11... | collective-permute-start | bytes 2752520 | tf_op jit(solution)/shard_map/ppermute | solution.py:446
  125.1 18.2 %collective-permute-start.2 = (f32[192,896]{1,0:T(8,128)}, f32[192,896]{1,0:T(8,128)}, u32[]{:S(2)}, u32[]{:S(2)}) collective-permute-start(f32[192,896]{1,0:T(8,128)} %get-tuple-element.62.own_ref), channel_id=1, source_target_pairs={{0,2},{1,3},{2,0},{3,1},{4,6},{5,7},{6,4},{7,5},{8,10},{9,11},{10,... | collective-permute-start | bytes 2064392 | tf_op jit(solution)/shard_map/ppermute | solution.py:446
  125.3 18.4 %collective-permute-start.9 = (f32[192,896]{1,0:T(8,128)}, f32[192,896]{1,0:T(8,128)}, u32[]{:S(2)}, u32[]{:S(2)}) collective-permute-start(f32[192,896]{1,0:T(8,128)} %get-tuple-element.62.own_ref), channel_id=1, source_target_pairs={{0,1},{1,0},{2,3},{3,2},{4,5},{5,4},{6,7},{7,6},{8,9},{9,8},{10,11... | collective-permute-start | bytes 2064392 | tf_op jit(solution)/shard_map/ppermute | solution.py:446
  143.2 2.5 %collective-permute-start.10 = (f32[192,896]{1,0:T(8,128)}, f32[192,896]{1,0:T(8,128)}, u32[]{:S(2)}, u32[]{:S(2)}) collective-permute-start(f32[192,896]{1,0:T(8,128)} %collective-permute-done.2.got_ref), channel_id=1, source_target_pairs={{0,1},{1,0},{2,3},{3,2},{4,5},{5,4},{6,7},{7,6},{8,9},{9,8},{10,11... | collective-permute-start | bytes 2064392 | tf_op jit(solution)/shard_map/ppermute | solution.py:446
  143.2 8.3 %collective-permute-start.1 = (f32[64,896]{1,0:T(8,128)}, f32[64,896]{1,0:T(8,128)}, u32[]{:S(2)}, u32[]{:S(2)}) collective-permute-start(f32[64,896]{1,0:T(8,128)} %get-tuple-element.61.own_ref), channel_id=1, source_target_pairs={{0,2},{1,3},{2,0},{3,1},{4,6},{5,7},{6,4},{7,5},{8,10},{9,11},{10,... | collective-permute-start | bytes 688136 | tf_op jit(solution)/shard_map/ppermute | solution.py:446
  143.5 9.3 %collective-permute-start.11 = (f32[64,896]{1,0:T(8,128)}, f32[64,896]{1,0:T(8,128)}, u32[]{:S(2)}, u32[]{:S(2)}) collective-permute-start(f32[64,896]{1,0:T(8,128)} %get-tuple-element.61.own_ref), channel_id=1, source_target_pairs={{0,1},{1,0},{2,3},{3,2},{4,5},{5,4},{6,7},{7,6},{8,9},{9,8},{10,11... | collective-permute-start | bytes 688136 | tf_op jit(solution)/shard_map/ppermute | solution.py:446
  151.6 1.8 %collective-permute-start.12 = (f32[64,896]{1,0:T(8,128)}, f32[64,896]{1,0:T(8,128)}, u32[]{:S(2)}, u32[]{:S(2)}) collective-permute-start(f32[64,896]{1,0:T(8,128)} %collective-permute-done.1.got_ref), channel_id=1, source_target_pairs={{0,1},{1,0},{2,3},{3,2},{4,5},{5,4},{6,7},{7,6},{8,9},{9,8},{10,11... | collective-permute-start | bytes 688136 | tf_op jit(solution)/shard_map/ppermute | solution.py:446
